TPU v7x, 256 devices: a whole 4x4x8 slice. The times are simulated.
256 devices in a mesh: track: 4 (over y), ifg: 4 (over z_lo), pix: 16 (over z_hi, x, core).
Axes of the slice: x: 4, y: 4, z: 8 (z_hi: 2, z_lo: 4; z = z_hi * 4 + z_lo), core: 2. Of those that a mesh axis runs over, the one named last changes fastest.
Arguments:
- phases: bfloat16 [4, 600, 262144], P('track', 'ifg', 'pix')
- pairs: int32 [4, 600, 2], P('track', 'ifg'), may hold values from 0 to 249, as said below
- date_map: int32 [4, 250], replicated, may hold values from 0 to 319, as said below
- knots: int32 [32], replicated, may hold values from 0 to 319, as said below
- look: float32 [4, 3, 262144], P(None, None, 'pix'), may hold values from -1 to 1
Outputs:
- enu: float32 [3, 320, 262144], P(None, None, ('pix', 'ifg', 'track'))
- spline: float32 [3, 32, 262144], P(None, None, ('pix', 'ifg', 'track'))
Inputs may be any that keep to these rules, and one draw needn't show every extreme that they name: pairs[t, k, 0] < pairs[t, k, 1] <= pairs[t, k, 0] + 5. `date_map`: the dates of one track map to distinct epochs. `knots`: strictly increasing, the first 0 and the last 319.
All inputs are finite; a program needn't handle non-finite values.
Results may differ from a plain program's by a relative error of at most 0.0003.
Values may be sent and summed in bfloat16 or wider, within the bound.
A program may use at most 128 MiB of HBM per device.

v0:
```python
import jax
import jax.numpy as jnp
from jax import lax
from jax.sharding import PartitionSpec as P

EPOCHS = 320


damping = 0.5
ridge = 0.1
HIGH = lax.Precision.HIGHEST


def joined_along(tiles, dim):
    tiles = jnp.moveaxis(tiles, 0, dim)
    lengths = tiles.shape
    return tiles.reshape(*lengths[:dim], lengths[dim] * lengths[dim + 1], *lengths[dim + 2 :])


def from_everyone(value, axis):
    copies = jnp.broadcast_to(value, (lax.axis_size(axis), *value.shape))
    return lax.all_to_all(copies, axis, split_axis=0, concat_axis=0, tiled=True)


def collect(value, axis, dim):
    return joined_along(from_everyone(value, axis), dim)


def taken_together(value, axis):
    everything = from_everyone(value, axis)
    return jnp.sum(everything, axis=0)


def incidence(pair_rows, ndate):
    dates = jnp.arange(ndate, dtype=jnp.int32)[:, None]
    later = (dates == pair_rows[None, :, 1]).astype(jnp.float32)
    earlier = (dates == pair_rows[None, :, 0]).astype(jnp.float32)
    return later - earlier


def inverse_normal(normal_part):
    ndate = normal_part.shape[0]
    normal = normal_part + damping * jnp.eye(ndate, dtype=jnp.float32)
    factor = jnp.linalg.cholesky(normal)
    return jax.scipy.linalg.cho_solve((factor, True), jnp.eye(ndate, dtype=jnp.float32))


def hat_basis(knots, n_epochs):
    spots = knots.astype(jnp.float32)
    left = jnp.concatenate([spots[:1] - 1.0, spots[:-1]])
    right = jnp.concatenate([spots[1:], spots[-1:] + 1.0])
    epochs = jnp.arange(n_epochs, dtype=jnp.float32)[:, None]
    rise = (epochs - left) / (spots - left)
    fall = (right - epochs) / (right - spots)
    return jnp.maximum(0.0, jnp.minimum(rise, fall))


def geometry(series, date_map, look, knots, n_epochs):
    epochs = jnp.arange(n_epochs, dtype=jnp.int32)
    onehot = (date_map[:, None, :] == epochs[None, :, None]).astype(jnp.float32)
    seen = jnp.sum(onehot, axis=2)
    resampled = jnp.einsum("tcd,tdp->tcp", onehot, series, precision=HIGH)

    def entry(first, second):
        value = jnp.einsum("tc,tp->cp", seen, look[:, first] * look[:, second], precision=HIGH)
        if first == second:
            value = value + ridge
        return value

    a00, a01, a02 = (entry(0, 0), entry(0, 1), entry(0, 2))
    a11, a12, a22 = (entry(1, 1), entry(1, 2), entry(2, 2))
    b_all = [jnp.sum(look[:, i][:, None, :] * resampled, axis=0) for i in range(3)]
    c00 = a11 * a22 - a12 * a12
    c01 = a02 * a12 - a01 * a22
    c02 = a01 * a12 - a02 * a11
    c11 = a00 * a22 - a02 * a02
    c12 = a01 * a02 - a00 * a12
    c22 = a00 * a11 - a01 * a01
    det = a00 * c00 + a01 * c01 + a02 * c02
    east = (c00 * b_all[0] + c01 * b_all[1] + c02 * b_all[2]) / det
    north = (c01 * b_all[0] + c11 * b_all[1] + c12 * b_all[2]) / det
    upward = (c02 * b_all[0] + c12 * b_all[1] + c22 * b_all[2]) / det
    enu = jnp.stack([east, north, upward])
    basis = hat_basis(knots, n_epochs)
    gram = jnp.dot(basis.T, basis, precision=HIGH)
    factor = jnp.linalg.cholesky(gram)
    fitter = jax.scipy.linalg.cho_solve((factor, True), basis.T)
    spline = jnp.einsum("kc,icp->ikp", fitter, enu, precision=HIGH)
    return (enu, spline)


def shards(phases, pairs, date_map, knots, look):
    ndate = date_map.shape[1]
    n_epochs = hat_count()
    n_track = lax.axis_size("track")
    n_ifg = lax.axis_size("ifg")
    width = phases.shape[2] // (n_track * n_ifg)
    offset = lax.axis_index("ifg") * (width * n_track) + lax.axis_index("track") * width
    look_local = lax.dynamic_slice_in_dim(look, offset, width, 2)
    phase_rows = phases[0]
    pair_rows = pairs[0]
    phase_all = lax.all_to_all(phase_rows, "ifg", split_axis=1, concat_axis=0, tiled=True)
    pair_all = collect(pair_rows, "ifg", 0)
    incid = incidence(pair_all, ndate)
    normal_part = jnp.dot(incid, incid.T, precision=HIGH)
    rhs = jnp.dot(incid.astype(jnp.bfloat16), phase_all, preferred_element_type=jnp.float32)
    ninv = inverse_normal(normal_part)
    pixel_count = rhs.shape[1] * lax.axis_size("ifg") * lax.axis_size("pix")
    series = jnp.dot(ninv, rhs, precision=HIGH)
    total = taken_together(jnp.sum(series, axis=1), ("ifg", "pix"))
    series = series - (total / pixel_count)[:, None]
    gathered = lax.all_to_all(series[None], "track", split_axis=2, concat_axis=0, tiled=True)
    return geometry(gathered, date_map, look_local, knots, n_epochs)


def hat_count():
    return EPOCHS


def solution(mesh):
    in_specs = (P("track", "ifg", "pix"), P("track", "ifg", None), P(), P(), P(None, None, "pix"))
    out_specs = (P(None, None, ("pix", "ifg", "track")), P(None, None, ("pix", "ifg", "track")))
    return jax.shard_map(shards, mesh=mesh, in_specs=in_specs, out_specs=out_specs, check_vma=False)
```

profile of v0, /device:TPU:1, one launch (start us, length us, event | category | flops | bytes accessed | tf_op | source)
XLA Modules:
  0.0 271.2 jit_solution(16111083648875466656)
XLA Ops:
  0.6 1.3 broadcast_in_dim.9
  1.9 6.4 %all-to-all-start = ((s32[4,150,2]{1,2,0:T(2,128)}), s32[4,150,2]{1,2,0:T(2,128)S(1)}, u32[]{:S(2)}, u32[]{:S(2)}) async-start(s32[4,150,2]{1,2,0:T(2,128)} %broadcast_in_dim.9), calls=%async_computation | async-start | bytes 16384 | tf_op jit(solution)/shard_map/all_to_all | solution.py:22
  8.3 11.1 %all_to_all.35 = bf16[150,4,4096]{2,1,0:T(4,128)(2,1)} reshape(bf16[1,150,16384]{2,1,0:T(8,128)(2,1)} %param.5) | data formatting | bytes 9830400 | tf_op jit(solution)/shard_map/all_to_all | solution.py:102
  19.4 7.3 %copy.30 = bf16[150,4,4096]{2,0,1:T(8,128)(2,1)} copy(bf16[150,4,4096]{2,1,0:T(4,128)(2,1)} %all_to_all.35) | data formatting | bytes 9830400 | tf_op jit(solution)/shard_map/all_to_all | solution.py:102
  26.8 5.6 %all-to-all-start.1 = ((bf16[150,4,4096]{2,0,1:T(8,128)(2,1)}), bf16[150,4,4096]{2,0,1:T(8,128)(2,1)}, u32[]{:S(2)}, u32[]{:S(2)}) async-start(bf16[150,4,4096]{2,0,1:T(8,128)(2,1)} %copy.30), calls=%async_computation.1 | async-start | bytes 9961472 | tf_op jit(solution)/shard_map/all_to_all | solution.py:102
  32.7 1.0 fusion.3
  33.9 11.7 %cholesky.63 = f32[128,128]{1,0:T(8,128)S(1)} custom-call(f32[128,128]{1,0:T(8,128)S(1)} %cholesky.156), custom_call_target="Cholesky" | custom-call | tf_op jit(solution)/shard_map/jit(cholesky)/cholesky | solution.py:44
  45.6 9.8 %custom-call.28 = f32[1,128,128]{1,2,0:T(8,128)S(1)} custom-call(f32[1,128,128]{2,1,0:T(8,128)S(1)} %get-tuple-element.40), custom_call_target="InvertDiagBlocksLowerTriangular" | custom-call | tf_op jit(solution)/shard_map/jit(cholesky)/cholesky | solution.py:44
  56.0 11.2 %cholesky.133 = f32[122,122]{1,0:T(8,128)S(1)} custom-call(f32[122,122]{1,0:T(8,128)S(1)} %convolution_subtract_fusion.2), custom_call_target="Cholesky" | custom-call | tf_op jit(solution)/shard_map/jit(cholesky)/cholesky | solution.py:44
  69.9 19.8 %custom-call.29 = f32[2,128,128]{1,2,0:T(8,128)S(1)} custom-call(f32[2,128,128]{2,1,0:T(8,128)S(1)} %pad_maximum_fusion.1), custom_call_target="InvertDiagBlocksLowerTriangular" | custom-call | tf_op jit(solution)/shard_map/jit(_cho_solve)/triangular_solve | solution.py:45
  91.5 50.6 %all-to-all-done.1 = bf16[150,4,4096]{2,0,1:T(8,128)(2,1)} async-done(((bf16[150,4,4096]{2,0,1:T(8,128)(2,1)}), bf16[150,4,4096]{2,0,1:T(8,128)(2,1)}, u32[]{:S(2)}, u32[]{:S(2)}) %all-to-all-start.1) | async-done | bytes 4915232 | tf_op jit(solution)/shard_map/all_to_all | solution.py:102
  142.1 6.0 %all_to_all.38 = bf16[600,4096]{1,0:T(8,128)(2,1)} reshape(bf16[4,150,4096]{2,1,0:T(8,128)(2,1)} %bitcast.11) | data formatting | bytes 9830400 | tf_op jit(solution)/shard_map/all_to_all | solution.py:102
  148.0 4.2 %fusion.5 = f32[250,4096]{1,0:T(8,128)S(1)} fusion(bf16[600,4096]{1,0:T(8,128)(2,1)} %all_to_all.38, s32[600]{0:T(1024)S(1)} %get-tuple-element.26, s32[600]{0:T(1024)S(1)} %get-tuple-element.25), kind=kOutput, calls=%fused_computation.31 | convolution fusion | flops 1229699968 | bytes 9016000 | tf_op jit(solution)/shard_map/dot_general | solution.py:106
  152.3 5.3 %fusion.48 = (f32[250]{0:T(256)S(1)}, f32[250,4096]{1,0:T(8,128)}) fusion(f32[250,4096]{1,0:T(8,128)S(1)} %fusion.5, f32[122,250]{1,0:T(8,128)S(1)} %fusion.26, f32[128,250]{1,0:T(8,128)S(1)} %fusion.25), kind=kOutput, calls=%fused_computation.113 | convolution fusion | flops 3073086208 | bytes 8443000 | tf_op jit(solution)/shard_map/dot_general | solution.py:109
  158.2 10.5 %all-to-all-start.2 = ((f32[64,1,250]{2,1,0:T(1,128)}), f32[64,1,250]{2,1,0:T(1,128)S(1)}, u32[]{:S(2)}, u32[]{:S(2)}) async-start(f32[64,1,250]{2,1,0:T(1,128)} %broadcast_in_dim.10), calls=%async_computation.2 | async-start | bytes 131072 | tf_op jit(solution)/shard_map/all_to_all | solution.py:22
  168.8 9.6 %all-to-all-done.2 = f32[64,1,250]{2,1,0:T(1,128)S(1)} async-done(((f32[64,1,250]{2,1,0:T(1,128)}), f32[64,1,250]{2,1,0:T(1,128)S(1)}, u32[]{:S(2)}, u32[]{:S(2)}) %all-to-all-start.2) | async-done | bytes 64032 | tf_op jit(solution)/shard_map/all_to_all | solution.py:22
  178.5 4.7 %subtract_bitcast_fusion = f32[1,250,4096]{2,1,0:T(8,128)} fusion(f32[250,4096]{1,0:T(8,128)} %get-tuple-element.50, f32[250]{0:T(256)S(1)} %broadcast_multiply_fusion), kind=kLoop, calls=%fused_computation.5 | loop fusion | flops 1024000 | bytes 8193000 | tf_op jit(solution)/shard_map/broadcast_in_dim | solution.py:112
  183.2 10.2 %copy.32 = f32[1,250,4096]{1,0,2:T(1,128)} copy(f32[1,250,4096]{2,1,0:T(8,128)} %subtract_bitcast_fusion) | data formatting | bytes 8192000 | tf_op jit(solution)/shard_map/broadcast_in_dim | solution.py:112
  193.4 5.1 %all-to-all-start.3 = ((f32[1,250,4096]{1,0,2:T(1,128)}), f32[1,250,4096]{1,0,2:T(1,128)}, u32[]{:S(2)}, u32[]{:S(2)}) async-start(f32[1,250,4096]{1,0,2:T(1,128)} %copy.32), calls=%async_computation.3 | async-start | bytes 8388608 | tf_op jit(solution)/shard_map/all_to_all | solution.py:112
  201.0 2.9 %cholesky.147 = f32[32,32]{1,0:T(8,128)S(1)} custom-call(f32[32,32]{1,0:T(8,128)S(1)} %fusion.33), custom_call_target="Cholesky" | custom-call | tf_op jit(solution)/shard_map/jit(cholesky)/cholesky | solution.py:86
  205.3 2.4 custom-call.30
  209.3 2.4 convolution_add_fusion
  211.7 2.4 convolution_add_fusion.1
  214.1 2.3 convolution_add_fusion.2
  216.4 1.2 fusion.35
  217.7 1.3 fusion.37
  218.9 28.1 %all-to-all-done.3 = f32[1,250,4096]{1,0,2:T(1,128)} async-done(((f32[1,250,4096]{1,0,2:T(1,128)}), f32[1,250,4096]{1,0,2:T(1,128)}, u32[]{:S(2)}, u32[]{:S(2)}) %all-to-all-start.3) | async-done | bytes 4096032 | tf_op jit(solution)/shard_map/all_to_all | solution.py:112
  247.1 4.4 %copy.35 = f32[1,250,4096]{1,2,0:T(8,128)} copy(f32[1,250,4096]{1,0,2:T(1,128)} %all-to-all-done.3) | data formatting | bytes 8192000
  251.5 5.6 %copy.33 = f32[1,250,4,1024]{3,1,2,0:T(8,128)} copy(f32[1,250,4,1024]{1,3,2,0:T(8,128)} %bitcast.84) | data formatting | bytes 8192000 | tf_op jit(solution)/shard_map/all_to_all | solution.py:112
  257.2 6.9 %multiply_reduce_fusion.2 = (f32[320,1024]{1,0:T(8,128)S(1)}, f32[320,1024]{1,0:T(8,128)S(1)}, f32[320,1024]{1,0:T(8,128)S(1)}) fusion(f32[4,1024]{1,0:T(4,128)S(1)} %get-tuple-element.36, f32[4,1024]{1,0:T(4,128)S(1)} %get-tuple-element.35, f32[4,1024]{1,0:T(4,128)S(1)} %get-tuple-element.34, f32[1,250,4,1024]{3,1,2,0:T(8,128)} %copy.33, ...), kind=kOutput, calls=%fused_computation.2 | convolution fusion | flops 3939361280 | bytes 8081312 | tf_op jit(solution)/shard_map/tcd,tdp->tcp/dot_general | solution.py:62
  264.1 3.0 %divide_bitcast_fusion.2 = (f32[1,320,1024]{2,1,0:T(8,128)S(1)}, f32[1,320,1024]{2,1,0:T(8,128)S(1)}, f32[1,320,1024]{2,1,0:T(8,128)S(1)}) fusion(f32[320,1024]{1,0:T(8,128)S(1)} %get-tuple-element.23, f32[320,1024]{1,0:T(8,128)S(1)} %get-tuple-element.24, f32[320,1024]{1,0:T(8,128)S(1)} %get-tuple-element.22, f32[320,1024]{1,0:T(8,128)S(1)} %copy-done.3, ...), kind=kOutput, calls=%fused_computation.13 | convolution fusion | flops 29167616 | bytes 14455808 | tf_op jit(solution)/shard_map/tc,tp->cp/dot_general | solution.py:65
  267.6 3.3 %convolution_bitcast_fusion = f32[3,32,1024]{2,1,0:T(8,128)} fusion(f32[3,320,1024]{2,1,0:T(8,128)S(1)} %pad_maximum_fusion, f32[32,320,1]{1,0,2:T(8,128)S(1)} %convolution_bitcast_fusion.1), kind=kOutput, calls=%fused_computation.20 | convolution fusion | flops 377487360 | bytes 4366336 | tf_op jit(solution)/shard_map/kc,icp->ikp/dot_general | solution.py:88
  (57 shorter events, 9.5 us)
Async XLA Ops:
  1.9 24.9 %all-to-all-start = ((s32[4,150,2]{1,2,0:T(2,128)}), s32[4,150,2]{1,2,0:T(2,128)S(1)}, u32[]{:S(2)}, u32[]{:S(2)}) async-start(s32[4,150,2]{1,2,0:T(2,128)} %broadcast_in_dim.9), calls=%async_computation | async-start | bytes 16384 | tf_op jit(solution)/shard_map/all_to_all | solution.py:22
  26.8 5.7 %copy-start.5 = (s32[32]{0:T(128)S(1)}, s32[32]{0:T(128)}, u32[]{:S(2)}) copy-start(s32[32]{0:T(128)} %param.8) | copy-start | bytes 388
  26.8 115.3 %all-to-all-start.1 = ((bf16[150,4,4096]{2,0,1:T(8,128)(2,1)}), bf16[150,4,4096]{2,0,1:T(8,128)(2,1)}, u32[]{:S(2)}, u32[]{:S(2)}) async-start(bf16[150,4,4096]{2,0,1:T(8,128)(2,1)} %copy.30), calls=%async_computation.1 | async-start | bytes 9961472 | tf_op jit(solution)/shard_map/all_to_all | solution.py:102
  158.2 20.2 %all-to-all-start.2 = ((f32[64,1,250]{2,1,0:T(1,128)}), f32[64,1,250]{2,1,0:T(1,128)S(1)}, u32[]{:S(2)}, u32[]{:S(2)}) async-start(f32[64,1,250]{2,1,0:T(1,128)} %broadcast_in_dim.10), calls=%async_computation.2 | async-start | bytes 131072 | tf_op jit(solution)/shard_map/all_to_all | solution.py:22
  193.4 53.6 %all-to-all-start.3 = ((f32[1,250,4096]{1,0,2:T(1,128)}), f32[1,250,4096]{1,0,2:T(1,128)}, u32[]{:S(2)}, u32[]{:S(2)}) async-start(f32[1,250,4096]{1,0,2:T(1,128)} %copy.32), calls=%async_computation.3 | async-start | bytes 8388608 | tf_op jit(solution)/shard_map/all_to_all | solution.py:112
  200.5 8.6 %copy-start.4 = (s32[4,250]{1,0:T(4,128)S(1)}, s32[4,250]{1,0:T(4,128)}, u32[]{:S(2)}) copy-start(s32[4,250]{1,0:T(4,128)} %param.7) | copy-start | bytes 12004
  257.1 6.9 %copy-start.1 = (f32[320,1024]{1,0:T(8,128)S(1)}, f32[320,1024]{1,0:T(8,128)}, u32[]{:S(2)}) copy-start(f32[320,1024]{1,0:T(8,128)} %convolution_add_fusion) | copy-start | bytes 3932164
  257.1 6.9 %copy-start.2 = (f32[320,1024]{1,0:T(8,128)S(1)}, f32[320,1024]{1,0:T(8,128)}, u32[]{:S(2)}) copy-start(f32[320,1024]{1,0:T(8,128)} %convolution_add_fusion.1) | copy-start | bytes 3932164
  257.1 6.9 %copy-start.3 = (f32[320,1024]{1,0:T(8,128)S(1)}, f32[320,1024]{1,0:T(8,128)}, u32[]{:S(2)}) copy-start(f32[320,1024]{1,0:T(8,128)} %convolution_add_fusion.2) | copy-start | bytes 3932164
  267.6 3.3 %copy-start = (f32[3,320,1024]{2,1,0:T(8,128)}, f32[3,320,1024]{2,1,0:T(8,128)S(1)}, u32[]{:S(2)}) copy-start(f32[3,320,1024]{2,1,0:T(8,128)S(1)} %pad_maximum_fusion) | copy-start | bytes 11796484
where the time goes:
time: 276 us; the launch traced here: 271 us
  waiting for transfers between devices  88.4 us (32%)
  other arithmetic  66.5 us (24%)
  local copies, waits for them, and re-layouts  48.4 us (18%)
  matrix products  36.4 us (13%)
  starting transfers between devices  27.6 us (10%)
  between operations  3.88 us (1%)
    all_to_all x1, waiting for transfers between devices, shards(): lax.all_to_all(phase_rows, 'ifg', split_axis=1, concat_axis=0, tiled=True)  50.6 us
    another operation x7, other arithmetic, inverse_normal(): factor = jnp.linalg.cholesky(normal)  34 us
    all_to_all x1, waiting for transfers between devices, shards(): lax.all_to_all(series[None], 'track', split_axis=2, concat_axis=0, tiled=...  28.1 us
    all_to_all x3, local copies, waits for them, and re-layouts, shards(): lax.all_to_all(phase_rows, 'ifg', split_axis=1, concat_axis=0, tiled=True)  24.4 us
    another operation x6, other arithmetic, inverse_normal(): jax.scipy.linalg.cho_solve((factor, True), jnp.eye(ndate, dtype=jnp.float...  20 us
    all_to_all x2, starting transfers between devices, from_everyone(): return lax.all_to_all(copies, axis, split_axis=0, concat_axis=0, tiled=True)  16.9 us
    dot_general x6, matrix products, entry(): jnp.einsum('tc,tp->cp', seen, look[:, first] * look[:, second], precision...  12.6 us
    broadcast_in_dim x1, local copies, waits for them, and re-layouts, shards(): series[None]  10.2 us
  transfers between devices with their start and end apart: 4, of which 3 were waited for; matrix products, arithmetic and copies ran while one was open for 31% of the time, Pallas kernels for 0%

commit v1 on v0

v1 whole, which is shorter than its diff:
```python
import functools

import jax
import jax.numpy as jnp
from jax import lax
from jax.experimental import pallas as pl
from jax.experimental.pallas import tpu as pltpu
from jax.sharding import PartitionSpec as P

EPOCHS = 320
MESH = pl.DeviceIdType.MESH
HIGH = lax.Precision.HIGHEST
F32 = jnp.float32
BF16 = jnp.bfloat16
damping = 0.5
ridge = 0.1
BAND = 8
PAIRS_OF = ((0, 0), (0, 1), (0, 2), (1, 1), (1, 2), (2, 2))


def dot(a, b, dims=((1,), (0,)), precision=None):
    return lax.dot_general(a, b, (dims, ((), ())), precision=precision, preferred_element_type=F32)


def iota(shape, dim):
    return lax.broadcasted_iota(jnp.int32, shape, dim)


def invert_small_blocks(blocks):
    rows, lanes = blocks.shape
    state = blocks.reshape(rows // BAND, BAND, lanes)
    sub = iota(state.shape, 1)
    lane = iota(state.shape, 2) % BAND
    for k in range(BAND):
        row = state[:, k : k + 1, :]
        col = state[:, :, k : k + 1]
        inv = 1.0 / row[:, :, k : k + 1]
        scaled = row * inv
        inner = state - col * scaled
        at_row = jnp.where(lane == k, jnp.broadcast_to(inv, state.shape), jnp.broadcast_to(scaled, state.shape))
        off_row = jnp.where(lane == k, -col * inv, inner)
        state = jnp.where(sub == k, at_row, off_row)
    return state.reshape(rows, lanes)


def invert_banded(matrix):
    n = matrix.shape[0]
    lanes = 128
    row, col = iota((n, n), 0), iota((n, n), 1)
    block_row, block_col = row // BAND, col // BAND
    eye = (row == col).astype(F32)
    fold = (iota((n, lanes), 0) % BAND == iota((n, lanes), 1) % BAND).astype(F32)
    stride, inverse_diag, basis = 1, jnp.zeros((n, n), F32), eye
    while True:
        last = stride * BAND >= n
        if last:
            here_row = block_row == 0
            here_col = block_col == 0
        else:
            here_row = block_row % (2 * stride) == stride
            here_col = block_col % (2 * stride) == stride
        on_diag = here_row & here_col & (block_row == block_col)
        blocks = dot(jnp.where(on_diag, matrix, jnp.where(here_row, 0.0, eye)), fold, precision=HIGH)
        small = invert_small_blocks(blocks)
        small = jnp.concatenate([small] * (n // lanes), axis=1)
        level_inverse = jnp.where(on_diag, small, 0.0)
        inverse_diag = inverse_diag + level_inverse
        if last:
            break
        rest_row = block_row % (2 * stride) == 0
        rest_col = block_col % (2 * stride) == 0
        step = jnp.where(here_row & rest_col, dot(level_inverse, matrix, precision=HIGH), 0.0)
        matrix = jnp.where(rest_row & rest_col, matrix - dot(matrix, step, precision=HIGH), 0.0)
        basis = basis - dot(basis, step, precision=HIGH)
        stride *= 2
    scaled = dot(basis, inverse_diag, precision=HIGH)
    return dot(scaled, basis, ((1,), (1,)), precision=HIGH)


def parts(value, count):
    out = []
    for _ in range(count):
        piece = value.astype(BF16)
        out.append(piece)
        value = value - piece.astype(F32)
    return out


def spline_fitter(knots_row, n_epochs, n_knots):
    lane = iota(knots_row.shape, 1)
    before = pltpu.roll(knots_row, 1, 1)
    after = pltpu.roll(knots_row, knots_row.shape[1] - 1, 1)
    left = jnp.where(lane == 0, knots_row - 1.0, before)
    right = jnp.where(lane == n_knots - 1, knots_row + 1.0, after)
    valid = lane < n_knots
    up = jnp.where(valid, knots_row - left, 1.0)
    down = jnp.where(valid, right - knots_row, 1.0)
    epochs = iota((n_epochs, knots_row.shape[1]), 0).astype(F32)
    hat = jnp.maximum(0.0, jnp.minimum((epochs - left) / up, (right - epochs) / down))
    basis = jnp.where(valid, hat, 0.0)
    size = knots_row.shape[1]
    gram = dot(basis, basis, ((0,), (0,)), precision=HIGH)
    row, col = iota((size, size), 0), iota((size, size), 1)
    gram = jnp.where((row == col) & (row >= n_knots), 1.0, gram)
    inverse = invert_banded(gram)
    return dot(inverse[:n_knots], basis, ((1,), (1,)), precision=HIGH)


def target_of(me, k, n):
    if n != 4:
        return lax.rem(me + k + 1, n)
    half = jnp.minimum(me, 3 - me)
    near = (1 - half) if k == 0 else k + 1
    return jnp.where(me < 2, near, 3 - near)


def exchange_kernel(
    sizes, phases, pairs, date_map, knots, look,
    gathered, fit_hi, fit_lo, picks, table, look_out,
    pair_all, own, landed, weights, incid, series, sums, totals, look_rows,
    own_sem, pair_send, pair_recv, look_sem, sum_send, sum_recv, total_send, total_recv, z_send, z_recv, y_send, y_recv, y_own,
):
    n_track, n_ifg, n_pix, widths, n_dates, n_epochs, n_knots = sizes
    track, ifg, pix = lax.axis_index("track"), lax.axis_index("ifg"), lax.axis_index("pix")
    count, pixels = phases.shape[1], phases.shape[2]
    quarter = pixels // n_ifg
    final = quarter // n_track
    padded = 8 * -(-n_dates // 8)
    while padded & (padded - 1):
        padded += 8
    padded = max(padded, 128)

    ifg_target = [target_of(ifg, k, n_ifg) for k in range(n_ifg - 1)]
    track_target = [lax.rem(track + k + 1, n_track) for k in range(n_track - 1)]

    barrier = pltpu.get_barrier_semaphore()
    for k in range(n_ifg - 1):
        pl.semaphore_signal(barrier, inc=1, device_id={"ifg": ifg_target[k]}, device_id_type=MESH)
    for k in range(n_track - 1):
        pl.semaphore_signal(barrier, inc=1, device_id={"track": track_target[k]}, device_id_type=MESH)
    for k in range(1, n_pix):
        pl.semaphore_signal(barrier, inc=1, device_id={"pix": lax.rem(pix + k, n_pix)}, device_id_type=MESH)
    pl.semaphore_wait(barrier, n_ifg + n_track + n_pix - 3)

    own_copy = pltpu.make_async_copy(phases.at[0], own, own_sem)
    own_copy.start()
    pair_copies = []
    for k in range(n_ifg - 1):
        pair_copies.append(pltpu.make_async_remote_copy(
            src_ref=pairs.at[0], dst_ref=pair_all.at[ifg], send_sem=pair_send.at[k], recv_sem=pair_recv.at[ifg],
            device_id={"ifg": ifg_target[k]}, device_id_type=MESH))
        pair_copies[-1].start()
    pltpu.make_async_copy(pairs.at[0], pair_all.at[ifg], pair_recv.at[ifg]).start()
    look_at = pl.multiple_of(ifg * quarter + track * final, final)
    look_in = pltpu.make_async_copy(look.at[:, :, pl.ds(look_at, final)], look_rows, look_sem.at[0])
    look_in.start()
    z_waits = []
    at = 0
    for j, width in enumerate(widths):
        for k in range(n_ifg - 1):
            for part in range(n_track):
                start = pl.multiple_of(ifg_target[k] * quarter + part * final + at, 128)
                pltpu.make_async_remote_copy(
                    src_ref=phases.at[0, :, pl.ds(start, width)],
                    dst_ref=landed.at[ifg, :, pl.ds(n_track * at + part * width, width)],
                    send_sem=z_send.at[k, j], recv_sem=z_recv.at[ifg, j],
                    device_id={"ifg": ifg_target[k]}, device_id_type=MESH).start()
        for part in range(n_track):
            start = pl.multiple_of(ifg * quarter + part * final + at, 128)
            pltpu.make_async_copy(
                phases.at[0, :, pl.ds(start, width)],
                landed.at[ifg, :, pl.ds(n_track * at + part * width, width)],
                z_recv.at[ifg, j]).start()
        at += width

    own_copy.wait()
    piece = 1024 if pixels % 1024 == 0 else pixels
    ones = jnp.ones((8, piece), BF16)

    def add_piece(k, total):
        return total + dot(ones, own[:, pl.ds(pl.multiple_of(k * piece, piece), piece)], ((1,), (1,)))

    own_sum = lax.fori_loop(0, pixels // piece, add_piece, jnp.zeros((8, count), F32))
    sums[0] = own_sum[:1]

    knots_row = jnp.concatenate([knots[...], jnp.zeros((1, 128 - n_knots), jnp.int32)], axis=1).astype(F32)
    fitter = spline_fitter(knots_row, n_epochs, n_knots)
    fit_hi[...], fit_lo[...] = parts(fitter, 2)

    sum_copies = []
    for k in range(1, n_pix):
        sum_copies.append(pltpu.make_async_remote_copy(
            src_ref=sums.at[0], dst_ref=sums.at[k], send_sem=sum_send.at[k], recv_sem=sum_recv.at[k],
            device_id={"pix": lax.rem(pix + k, n_pix)}, device_id_type=MESH))
        sum_copies[-1].start()

    code = jnp.zeros((n_epochs, 1), jnp.int32)
    for t in range(n_track):
        hit = (iota((n_epochs, n_dates), 0) == date_map[t : t + 1, :]).astype(F32)
        code = code + (jnp.max(hit, axis=1, keepdims=True) > 0.5).astype(jnp.int32) * (1 << t)
    n_masks = 1 << n_track
    lane = iota((n_epochs, 3 * n_masks), 1)
    picks[...] = (lane % n_masks == code).astype(F32).astype(BF16)

    look_in.wait()
    look_out[...] = look_rows[...]
    mask = iota((n_masks, final), 0)
    bits = [((mask >> t) & 1).astype(F32) for t in range(n_track)]

    def entry(i, j):
        value = ridge if i == j else 0.0
        for t in range(n_track):
            value = value + bits[t] * (look_rows[i, t : t + 1, :] * look_rows[j, t : t + 1, :])
        return value

    a00, a01, a02, a11, a12, a22 = [entry(i, j) for i, j in PAIRS_OF]
    c00 = a11 * a22 - a12 * a12
    c01 = a02 * a12 - a01 * a22
    c02 = a01 * a12 - a02 * a11
    c11 = a00 * a22 - a02 * a02
    c12 = a01 * a02 - a00 * a12
    c22 = a00 * a11 - a01 * a01
    det = a00 * c00 + a01 * c01 + a02 * c02
    for e, cofactor in enumerate((c00, c01, c02, c11, c12, c22)):
        table[e] = jnp.concatenate(parts(cofactor / det, 3), axis=0)

    for s in range(n_ifg):
        pltpu.make_async_copy(pair_all.at[s], pair_all.at[s], pair_recv.at[s]).wait()
    normal = jnp.zeros((padded, padded), F32)
    dates = iota((padded, count), 0)
    for s in range(n_ifg):
        rows = pair_all[s]
        matrix = (dates == rows[1:2, :]).astype(F32) - (dates == rows[0:1, :]).astype(F32)
        incid[s] = matrix
        matrix = matrix.astype(BF16)
        normal = normal + dot(matrix, matrix, ((1,), (1,)))
    normal = normal + jnp.where(iota(normal.shape, 0) == iota(normal.shape, 1), damping, 0.0)
    inverse = invert_banded(normal)

    total = sums[0]
    for k in range(1, n_pix):
        pltpu.make_async_copy(sums.at[k], sums.at[k], sum_recv.at[k]).wait()
        total = total + sums[k]
    totals[ifg] = total

    my_map = date_map[pl.ds(track, 1), :]
    placed = (iota((n_epochs, n_dates), 0) == my_map).astype(F32)
    placed = dot(placed, inverse[:n_dates], precision=HIGH)
    for s in range(n_ifg):
        weight = dot(placed, incid[s], precision=HIGH)
        weights[s, 0], weights[s, 1] = parts(weight, 2)
    total_copies = []
    for k in range(n_ifg - 1):
        total_copies.append(pltpu.make_async_remote_copy(
            src_ref=totals.at[ifg], dst_ref=totals.at[ifg], send_sem=total_send.at[k], recv_sem=total_recv.at[ifg],
            device_id={"ifg": ifg_target[k]}, device_id_type=MESH))
        total_copies[-1].start()
    for k in range(n_ifg - 1):
        s = ifg_target[k]
        pltpu.make_async_copy(totals.at[s], totals.at[s], total_recv.at[s]).wait()
    mean = jnp.zeros((n_epochs, 1), F32)
    for s in range(n_ifg):
        weight = weights[s, 0].astype(F32) + weights[s, 1].astype(F32)
        mean = mean + jnp.sum(weight * totals[s], axis=1, keepdims=True)
    mean = mean / (pixels * n_pix)

    at = 0
    for j, width in enumerate(widths):
        for s in range(n_ifg):
            chunk = landed.at[s, :, pl.ds(n_track * at, n_track * width)]
            pltpu.make_async_copy(chunk, chunk, z_recv.at[s, j]).wait()
        for k in range(n_track):
            part = track_target[k] if k < n_track - 1 else track
            where = pl.multiple_of(n_track * at + part * width, 128)
            value = jnp.zeros((n_epochs, width), F32)
            for s in range(n_ifg):
                phase = landed[s, :, pl.ds(where, width)]
                value = value + dot(weights[s, 0], phase) + dot(weights[s, 1], phase)
            series[:, pl.ds(where, width)] = value - mean
            if k < n_track - 1:
                pltpu.make_async_remote_copy(
                    src_ref=series.at[:, pl.ds(where, width)], dst_ref=gathered.at[track, :, pl.ds(at, width)],
                    send_sem=y_send.at[k, j], recv_sem=y_recv.at[track, j],
                    device_id={"track": part}, device_id_type=MESH).start()
            else:
                pltpu.make_async_copy(
                    series.at[:, pl.ds(where, width)], gathered.at[track, :, pl.ds(at, width)], y_recv.at[track, j]).start()
        at += width

    for copy in pair_copies + sum_copies + total_copies:
        copy.wait_send()
    at = 0
    for j, width in enumerate(widths):
        for k in range(n_ifg - 1):
            chunk = landed.at[0, :, pl.ds(n_track * at, n_track * width)]
            pltpu.make_async_copy(chunk, chunk, z_send.at[k, j]).wait()
        for t in range(n_track):
            here = gathered.at[t, :, pl.ds(at, width)]
            pltpu.make_async_copy(here, here, y_recv.at[t, j]).wait()
        for k in range(n_track - 1):
            here = series.at[:, pl.ds(0, width)]
            pltpu.make_async_copy(here, here, y_send.at[k, j]).wait()
        at += width


def geometry_kernel(gathered, fit_hi, fit_lo, picks, table, look, enu, spline):
    n_track = gathered.shape[0]
    select = picks[...]
    entries = {}
    for e, (i, j) in enumerate(PAIRS_OF):
        entries[i, j] = entries[j, i] = dot(select, table[e])
    right = []
    for i in range(3):
        value = look[i, 0:1, :] * gathered[0]
        for t in range(1, n_track):
            value = value + look[i, t : t + 1, :] * gathered[t]
        right.append(value)
    for i in range(3):
        value = entries[i, 0] * right[0] + entries[i, 1] * right[1] + entries[i, 2] * right[2]
        enu[i] = value
        hi, lo = parts(value, 2)
        spline[i] = dot(fit_hi[...], hi) + dot(fit_hi[...], lo) + dot(fit_lo[...], hi)


def chunk_widths(final):
    if final == 1024:
        return (256, 256, 256, 128, 128)
    return (final // 2, final // 2) if final % 256 == 0 else (final,)


def shards(phases, pairs, date_map, knots, look):
    n_track, n_ifg, n_pix = lax.axis_size("track"), lax.axis_size("ifg"), lax.axis_size("pix")
    count, pixels = phases.shape[1], phases.shape[2]
    quarter = pixels // n_ifg
    final = quarter // n_track
    n_dates, n_epochs, n_knots = date_map.shape[1], EPOCHS, knots.shape[0]
    widths = chunk_widths(final)
    n = len(widths)
    padded = 128
    while padded < n_dates:
        padded *= 2
    n_masks = 1 << n_track
    sizes = (n_track, n_ifg, n_pix, widths, n_dates, n_epochs, n_knots)
    vmem = pl.BlockSpec(memory_space=pltpu.VMEM)
    anywhere = pl.BlockSpec(memory_space=pl.ANY)
    dma = pltpu.SemaphoreType.DMA
    gathered, fit_hi, fit_lo, picks, table, look_local = pl.pallas_call(
        functools.partial(exchange_kernel, sizes),
        out_shape=(
            jax.ShapeDtypeStruct((n_track, n_epochs, final), F32),
            jax.ShapeDtypeStruct((n_knots, n_epochs), BF16),
            jax.ShapeDtypeStruct((n_knots, n_epochs), BF16),
            jax.ShapeDtypeStruct((n_epochs, 3 * n_masks), BF16),
            jax.ShapeDtypeStruct((len(PAIRS_OF), 3 * n_masks, final), BF16),
            jax.ShapeDtypeStruct((3, n_track, final), F32),
        ),
        in_specs=[anywhere, anywhere, vmem, vmem, anywhere],
        out_specs=(anywhere, vmem, vmem, vmem, vmem, vmem),
        scratch_shapes=[
            pltpu.VMEM((n_ifg, 2, count), jnp.int32),
            pltpu.VMEM((count, pixels), BF16),
            pltpu.VMEM((n_ifg, count, quarter), BF16),
            pltpu.VMEM((n_ifg, 2, n_epochs, count), BF16),
            pltpu.VMEM((n_ifg, padded, count), F32),
            pltpu.VMEM((n_epochs, quarter), F32),
            pltpu.VMEM((n_pix, 1, count), F32),
            pltpu.VMEM((n_ifg, 1, count), F32),
            pltpu.VMEM((3, n_track, final), F32),
            dma(()), dma((n_ifg,)), dma((n_ifg,)), dma((1,)),
            dma((n_pix,)), dma((n_pix,)), dma((n_ifg,)), dma((n_ifg,)),
            dma((n_ifg, n)), dma((n_ifg, n)), dma((n_track, n)), dma((n_track, n)), dma(()),
        ],
        compiler_params=pltpu.CompilerParams(collective_id=0, has_side_effects=True, vmem_limit_bytes=56 << 20),
        name="exchange",
    )(phases, jnp.transpose(pairs, (0, 2, 1)), date_map, knots[None, :], jnp.transpose(look, (1, 0, 2)))
    width = min(final, 256)
    enu, spline = pl.pallas_call(
        geometry_kernel,
        grid=(final // width,),
        out_shape=(
            jax.ShapeDtypeStruct((3, n_epochs, final), F32),
            jax.ShapeDtypeStruct((3, n_knots, final), F32),
        ),
        in_specs=[
            pl.BlockSpec((n_track, n_epochs, width), lambda g: (0, 0, g)),
            pl.BlockSpec((n_knots, n_epochs), lambda g: (0, 0)),
            pl.BlockSpec((n_knots, n_epochs), lambda g: (0, 0)),
            pl.BlockSpec((n_epochs, 3 * n_masks), lambda g: (0, 0)),
            pl.BlockSpec((len(PAIRS_OF), 3 * n_masks, width), lambda g: (0, 0, g)),
            pl.BlockSpec((3, n_track, width), lambda g: (0, 0, g)),
        ],
        out_specs=(
            pl.BlockSpec((3, n_epochs, width), lambda g: (0, 0, g)),
            pl.BlockSpec((3, n_knots, width), lambda g: (0, 0, g)),
        ),
        compiler_params=pltpu.CompilerParams(vmem_limit_bytes=56 << 20),
        name="geometry",
    )(gathered, fit_hi, fit_lo, picks, table, look_local)
    return enu, spline


def solution(mesh):
    in_specs = (P("track", "ifg", "pix"), P("track", "ifg", None), P(), P(), P(None, None, "pix"))
    out_specs = (P(None, None, ("pix", "ifg", "track")), P(None, None, ("pix", "ifg", "track")))
    return jax.shard_map(shards, mesh=mesh, in_specs=in_specs, out_specs=out_specs, check_vma=False)
```

time: 276 us -> 191 us (0.69); the launches traced: 271 us -> 191 us
  Pallas kernels: 0 us -> 190 us
  waiting for transfers between devices: 88.4 us -> 0 us
  other arithmetic: 66.5 us -> 0 us
  local copies, waits for them, and re-layouts: 48.4 us -> 0 us
  matrix products: 36.4 us -> 0 us
  starting transfers between devices: 27.6 us -> 0 us
  between operations: 3.88 us -> 0.64 us
    pallas_call x0 -> x2, Pallas kernels: none -> 190 us  [the longest x1 184 us: shards(): pl.pallas_call(functools.partial(exchange_kernel, sizes), out_shape=(jax....]
    all_to_all x4 -> x0, waiting for transfers between devices: 88.4 us -> none  [the longest x1 50.6 us: shards(): lax.all_to_all(phase_rows, 'ifg', split_axis=1, concat_axis=0, tiled=True)]
    another operation x19 -> x0, other arithmetic: 61.2 us -> none  [the longest x7 34 us: inverse_normal(): factor = jnp.linalg.cholesky(normal)]
    dot_general x12 -> x0, matrix products: 33.8 us -> none  [the longest x6 12.6 us: entry(): jnp.einsum('tc,tp->cp', seen, look[:, first] * look[:, second], precision...]
    all_to_all x5 -> x0, local copies, waits for them, and re-layouts: 30 us -> none  [the longest x3 24.4 us: shards(): lax.all_to_all(phase_rows, 'ifg', split_axis=1, concat_axis=0, tiled=True)]
    all_to_all x4 -> x0, starting transfers between devices: 27.6 us -> none  [the longest x2 16.9 us: from_everyone(): return lax.all_to_all(copies, axis, split_axis=0, concat_axis=0, tiled=True)]
    broadcast_in_dim x3 -> x0, local copies, waits for them, and re-layouts: 12.2 us -> none  [the longest x1 10.2 us: shards(): series[None]]
    broadcast_in_dim x1 -> x0, other arithmetic: 4.7 us -> none  [shards(): series[None]]
  transfers between devices with their start and end apart: 4 -> 0, of which waited for: 3 -> 0; matrix products, arithmetic and copies ran while one was open for 31% -> 0% of each run, Pallas kernels for 0% -> 0%
where the time goes in v1:
time: 191 us
  Pallas kernels  190 us (99%)
    pallas_call x1, Pallas kernels, shards(): pl.pallas_call(functools.partial(exchange_kernel, sizes), out_shape=(jax....  184 us
    pallas_call x1, Pallas kernels, shards(): pl.pallas_call(geometry_kernel, grid=(final // width,), out_shape=(jax.Sh...  6.6 us

profile of v1, /device:TPU:1, one launch (start us, length us, event | category | flops | bytes accessed | tf_op | source)
XLA Modules:
  0.0 191.0 jit_solution(12196303759075237938)
XLA Ops:
  0.6 183.8 %exchange.1 = (f32[4,320,1024]{2,1,0:T(8,128)}, bf16[32,320]{1,0:T(8,128)(2,1)}, bf16[32,320]{1,0:T(8,128)(2,1)}, bf16[320,48]{1,0:T(8,128)(2,1)}, bf16[6,48,1024]{2,1,0:T(8,128)(2,1)}, /*index=5*/f32[3,4,1024]{2,1,0:T(4,128)}) custom-call(bf16[1,150,16384]{2,1,0:T(8,128)(2,1)} %phases.1, s32[1,2,150]{2,1,0:T(2,128)} %bitcast.4, s32[4,250]{1,0:T(4,128)} %date_map.1, ...), custom_call_target="tpu_custom_call" | custom-call | tf_op jit(solution)/shard_map/exchange/pallas_call | solution.py:347
  184.4 6.6 %geometry.1 = (f32[3,320,1024]{2,1,0:T(8,128)}, f32[3,32,1024]{2,1,0:T(8,128)}) custom-call(f32[4,320,1024]{2,1,0:T(8,128)} %get-tuple-element.8.gathered, bf16[32,320]{1,0:T(8,128)(2,1)} %get-tuple-element.9.fit_hi, bf16[32,320]{1,0:T(8,128)(2,1)} %get-tuple-element.10.fit_lo, bf16[320,48]{1,0:T(8,128)(2,1)} %get-tuple-element.11.picks, ...), custom_call_target="tpu_custom_call" | custom-call | tf_op jit(solution)/shard_map/geometry/pallas_call | solution.py:377

commit v2 on v1

--- a/solution.py
+++ b/solution.py
@@ -116,9 +116,9 @@
 
 def exchange_kernel(
     sizes, phases, pairs, date_map, knots, look,
-    gathered, fit_hi, fit_lo, picks, table, look_out,
-    pair_all, own, landed, weights, incid, series, sums, totals, look_rows,
-    own_sem, pair_send, pair_recv, look_sem, sum_send, sum_recv, total_send, total_recv, z_send, z_recv, y_send, y_recv, y_own,
+    gathered, fit_hi, fit_lo, picks, table, look_out, mean_out,
+    pair_all, own, landed, weights, incid, series, sums, totals, means, look_rows,
+    own_sem, pair_send, pair_recv, look_sem, sum_send, sum_recv, total_send, total_recv, mean_send, mean_recv, z_send, z_recv, y_send, y_recv,
 ):
     n_track, n_ifg, n_pix, widths, n_dates, n_epochs, n_knots = sizes
     track, ifg, pix = lax.axis_index("track"), lax.axis_index("ifg"), lax.axis_index("pix")
@@ -154,9 +154,10 @@
     look_at = pl.multiple_of(ifg * quarter + track * final, final)
     look_in = pltpu.make_async_copy(look.at[:, :, pl.ds(look_at, final)], look_rows, look_sem.at[0])
     look_in.start()
-    z_waits = []
-    at = 0
-    for j, width in enumerate(widths):
+    starts = [sum(widths[:j]) for j in range(len(widths))]
+
+    def send_chunk(j):
+        at, width = starts[j], widths[j]
         for k in range(n_ifg - 1):
             for part in range(n_track):
                 start = pl.multiple_of(ifg_target[k] * quarter + part * final + at, 128)
@@ -171,7 +172,10 @@
                 phases.at[0, :, pl.ds(start, width)],
                 landed.at[ifg, :, pl.ds(n_track * at + part * width, width)],
                 z_recv.at[ifg, j]).start()
-        at += width
+
+    batches = (1, min(3, len(widths)), len(widths))
+    for j in range(batches[0]):
+        send_chunk(j)
 
     own_copy.wait()
     piece = 1024 if pixels % 1024 == 0 else pixels
@@ -182,17 +186,6 @@
 
     own_sum = lax.fori_loop(0, pixels // piece, add_piece, jnp.zeros((8, count), F32))
     sums[0] = own_sum[:1]
-
-    knots_row = jnp.concatenate([knots[...], jnp.zeros((1, 128 - n_knots), jnp.int32)], axis=1).astype(F32)
-    fitter = spline_fitter(knots_row, n_epochs, n_knots)
-    fit_hi[...], fit_lo[...] = parts(fitter, 2)
-
-    sum_copies = []
-    for k in range(1, n_pix):
-        sum_copies.append(pltpu.make_async_remote_copy(
-            src_ref=sums.at[0], dst_ref=sums.at[k], send_sem=sum_send.at[k], recv_sem=sum_recv.at[k],
-            device_id={"pix": lax.rem(pix + k, n_pix)}, device_id_type=MESH))
-        sum_copies[-1].start()
 
     code = jnp.zeros((n_epochs, 1), jnp.int32)
     for t in range(n_track):
@@ -201,6 +194,19 @@
     n_masks = 1 << n_track
     lane = iota((n_epochs, 3 * n_masks), 1)
     picks[...] = (lane % n_masks == code).astype(F32).astype(BF16)
+
+    sum_copies = []
+    for k in range(1, n_pix):
+        sum_copies.append(pltpu.make_async_remote_copy(
+            src_ref=sums.at[0], dst_ref=sums.at[k], send_sem=sum_send.at[k], recv_sem=sum_recv.at[k],
+            device_id={"pix": lax.rem(pix + k, n_pix)}, device_id_type=MESH))
+        sum_copies[-1].start()
+    for j in range(batches[0], batches[1]):
+        send_chunk(j)
+
+    knots_row = jnp.concatenate([knots[...], jnp.zeros((1, 128 - n_knots), jnp.int32)], axis=1).astype(F32)
+    fitter = spline_fitter(knots_row, n_epochs, n_knots)
+    fit_hi[...], fit_lo[...] = parts(fitter, 2)
 
     look_in.wait()
     look_out[...] = look_rows[...]
@@ -255,17 +261,29 @@
             src_ref=totals.at[ifg], dst_ref=totals.at[ifg], send_sem=total_send.at[k], recv_sem=total_recv.at[ifg],
             device_id={"ifg": ifg_target[k]}, device_id_type=MESH))
         total_copies[-1].start()
-    for k in range(n_ifg - 1):
-        s = ifg_target[k]
-        pltpu.make_async_copy(totals.at[s], totals.at[s], total_recv.at[s]).wait()
-    mean = jnp.zeros((n_epochs, 1), F32)
-    for s in range(n_ifg):
-        weight = weights[s, 0].astype(F32) + weights[s, 1].astype(F32)
-        mean = mean + jnp.sum(weight * totals[s], axis=1, keepdims=True)
-    mean = mean / (pixels * n_pix)
-
+    for j in range(batches[1], batches[2]):
+        send_chunk(j)
+
+    def send_mean():
+        for k in range(n_ifg - 1):
+            s = ifg_target[k]
+            pltpu.make_async_copy(totals.at[s], totals.at[s], total_recv.at[s]).wait()
+        mean = jnp.zeros((1, n_epochs), F32)
+        for s in range(n_ifg):
+            weight = weights[s, 0].astype(F32) + weights[s, 1].astype(F32)
+            mean = mean + dot(totals[s], weight, ((1,), (1,)), precision=HIGH)
+        means[track] = mean / (pixels * n_pix)
+        for k in range(n_track - 1):
+            mean_copies.append(pltpu.make_async_remote_copy(
+                src_ref=means.at[track], dst_ref=means.at[track], send_sem=mean_send.at[k], recv_sem=mean_recv.at[track],
+                device_id={"track": track_target[k]}, device_id_type=MESH))
+            mean_copies[-1].start()
+
+    mean_copies = []
     at = 0
     for j, width in enumerate(widths):
+        if j == len(widths) - 1:
+            send_mean()
         for s in range(n_ifg):
             chunk = landed.at[s, :, pl.ds(n_track * at, n_track * width)]
             pltpu.make_async_copy(chunk, chunk, z_recv.at[s, j]).wait()
@@ -276,7 +294,7 @@
             for s in range(n_ifg):
                 phase = landed[s, :, pl.ds(where, width)]
                 value = value + dot(weights[s, 0], phase) + dot(weights[s, 1], phase)
-            series[:, pl.ds(where, width)] = value - mean
+            series[:, pl.ds(where, width)] = value
             if k < n_track - 1:
                 pltpu.make_async_remote_copy(
                     src_ref=series.at[:, pl.ds(where, width)], dst_ref=gathered.at[track, :, pl.ds(at, width)],
@@ -287,7 +305,14 @@
                     series.at[:, pl.ds(where, width)], gathered.at[track, :, pl.ds(at, width)], y_recv.at[track, j]).start()
         at += width
 
-    for copy in pair_copies + sum_copies + total_copies:
+    for k in range(n_track - 1):
+        t = track_target[k]
+        pltpu.make_async_copy(means.at[t], means.at[t], mean_recv.at[t]).wait()
+    eye = (iota((n_epochs, n_epochs), 0) == iota((n_epochs, n_epochs), 1)).astype(F32)
+    mean_out[...] = jnp.concatenate(
+        [dot(eye, means[t], ((1,), (1,)), precision=HIGH) for t in range(n_track)], axis=1)
+
+    for copy in pair_copies + sum_copies + total_copies + mean_copies:
         copy.wait_send()
     at = 0
     for j, width in enumerate(widths):
@@ -303,17 +328,18 @@
         at += width
 
 
-def geometry_kernel(gathered, fit_hi, fit_lo, picks, table, look, enu, spline):
+def geometry_kernel(gathered, fit_hi, fit_lo, picks, table, look, means, enu, spline):
     n_track = gathered.shape[0]
     select = picks[...]
     entries = {}
     for e, (i, j) in enumerate(PAIRS_OF):
         entries[i, j] = entries[j, i] = dot(select, table[e])
+    tracks = [gathered[t] - means[:, t : t + 1] for t in range(n_track)]
     right = []
     for i in range(3):
-        value = look[i, 0:1, :] * gathered[0]
+        value = look[i, 0:1, :] * tracks[0]
         for t in range(1, n_track):
-            value = value + look[i, t : t + 1, :] * gathered[t]
+            value = value + look[i, t : t + 1, :] * tracks[t]
         right.append(value)
     for i in range(3):
         value = entries[i, 0] * right[0] + entries[i, 1] * right[1] + entries[i, 2] * right[2]
@@ -344,7 +370,7 @@
     vmem = pl.BlockSpec(memory_space=pltpu.VMEM)
     anywhere = pl.BlockSpec(memory_space=pl.ANY)
     dma = pltpu.SemaphoreType.DMA
-    gathered, fit_hi, fit_lo, picks, table, look_local = pl.pallas_call(
+    gathered, fit_hi, fit_lo, picks, table, look_local, means = pl.pallas_call(
         functools.partial(exchange_kernel, sizes),
         out_shape=(
             jax.ShapeDtypeStruct((n_track, n_epochs, final), F32),
@@ -353,9 +379,10 @@
             jax.ShapeDtypeStruct((n_epochs, 3 * n_masks), BF16),
             jax.ShapeDtypeStruct((len(PAIRS_OF), 3 * n_masks, final), BF16),
             jax.ShapeDtypeStruct((3, n_track, final), F32),
+            jax.ShapeDtypeStruct((n_epochs, n_track), F32),
         ),
         in_specs=[anywhere, anywhere, vmem, vmem, anywhere],
-        out_specs=(anywhere, vmem, vmem, vmem, vmem, vmem),
+        out_specs=(anywhere,) + (vmem,) * 6,
         scratch_shapes=[
             pltpu.VMEM((n_ifg, 2, count), jnp.int32),
             pltpu.VMEM((count, pixels), BF16),
@@ -365,10 +392,11 @@
             pltpu.VMEM((n_epochs, quarter), F32),
             pltpu.VMEM((n_pix, 1, count), F32),
             pltpu.VMEM((n_ifg, 1, count), F32),
+            pltpu.VMEM((n_track, 1, n_epochs), F32),
             pltpu.VMEM((3, n_track, final), F32),
             dma(()), dma((n_ifg,)), dma((n_ifg,)), dma((1,)),
             dma((n_pix,)), dma((n_pix,)), dma((n_ifg,)), dma((n_ifg,)),
-            dma((n_ifg, n)), dma((n_ifg, n)), dma((n_track, n)), dma((n_track, n)), dma(()),
+            dma((n_track,)), dma((n_track,)), dma((n_ifg, n)), dma((n_ifg, n)), dma((n_track, n)), dma((n_track, n)),
         ],
         compiler_params=pltpu.CompilerParams(collective_id=0, has_side_effects=True, vmem_limit_bytes=56 << 20),
         name="exchange",
@@ -388,6 +416,7 @@
             pl.BlockSpec((n_epochs, 3 * n_masks), lambda g: (0, 0)),
             pl.BlockSpec((len(PAIRS_OF), 3 * n_masks, width), lambda g: (0, 0, g)),
             pl.BlockSpec((3, n_track, width), lambda g: (0, 0, g)),
+            pl.BlockSpec((n_epochs, n_track), lambda g: (0, 0)),
         ],
         out_specs=(
             pl.BlockSpec((3, n_epochs, width), lambda g: (0, 0, g)),
@@ -395,7 +424,7 @@
         ),
         compiler_params=pltpu.CompilerParams(vmem_limit_bytes=56 << 20),
         name="geometry",
-    )(gathered, fit_hi, fit_lo, picks, table, look_local)
+    )(gathered, fit_hi, fit_lo, picks, table, look_local, means)
     return enu, spline
 
 

time: 191 us -> 150 us (0.79)
  Pallas kernels: 190 us -> 149 us
    pallas_call x1, Pallas kernels: 184 us -> 142 us  [shards(): pl.pallas_call(functools.partial(exchange_kernel, sizes), out_shape=(jax....]
where the time goes in v2:
time: 150 us; the launch traced here: 149 us
  Pallas kernels  149 us (99%)
    pallas_call x1, Pallas kernels, shards(): pl.pallas_call(functools.partial(exchange_kernel, sizes), out_shape=(jax....  142 us
    pallas_call x1, Pallas kernels, shards(): pl.pallas_call(geometry_kernel, grid=(final // width,), out_shape=(jax.Sh...  7 us

profile of v2, /device:TPU:1, one launch (start us, length us, event | category | flops | bytes accessed | tf_op | source)
XLA Modules:
  0.0 149.2 jit_solution(6263522711801391016)
XLA Ops:
  0.6 141.6 %exchange.1 = (f32[4,320,1024]{2,1,0:T(8,128)}, bf16[32,320]{1,0:T(8,128)(2,1)}, bf16[32,320]{1,0:T(8,128)(2,1)}, bf16[320,48]{1,0:T(8,128)(2,1)}, bf16[6,48,102...) custom-call(bf16[1,150,16384]{2,1,0:T(8,128)(2,1)} %phases.1, s32[1,2,150]{2,1,0:T(2,128)} %bitcast.4, ...), custom_call_target="tpu_custom_call" | custom-call | tf_op jit(solution)/shard_map/exchange/pallas_call | solution.py:373
  142.2 7.0 %geometry.1 = (f32[3,320,1024]{2,1,0:T(8,128)}, f32[3,32,1024]{2,1,0:T(8,128)}) custom-call(f32[4,320,1024]{2,1,0:T(8,128)} %get-tuple-element.9.gathered, bf16[32,320]{1,0:T(8,128)(2,1)} %get-tuple-element.10.fit_hi, bf16[32,320]{1,0:T(8,128)(2,1)} %get-tuple-element.11.fit_lo, bf16[320,48]{1,0:T(8,128)(2,1)} %get-tuple-element.12.picks, ...), custom_call_target="tpu_custom_call" | custom-call | tf_op jit(solution)/shard_map/geometry/pallas_call | solution.py:405

commit v3 on v2

--- a/solution.py
+++ b/solution.py
@@ -116,7 +116,7 @@
 
 def exchange_kernel(
     sizes, phases, pairs, date_map, knots, look,
-    gathered, fit_hi, fit_lo, picks, table, look_out, mean_out,
+    gathered, fit, picks, table, look_out, mean_out,
     pair_all, own, landed, weights, incid, series, sums, totals, means, look_rows,
     own_sem, pair_send, pair_recv, look_sem, sum_send, sum_recv, total_send, total_recv, mean_send, mean_recv, z_send, z_recv, y_send, y_recv,
 ):
@@ -131,7 +131,9 @@
     padded = max(padded, 128)
 
     ifg_target = [target_of(ifg, k, n_ifg) for k in range(n_ifg - 1)]
-    track_target = [lax.rem(track + k + 1, n_track) for k in range(n_track - 1)]
+    steps = sorted(range(1, n_track), key=lambda k: -min(k, n_track - k))
+    track_target = [lax.rem(track + k, n_track) for k in steps]
+    parts_order = track_target + [track]
 
     barrier = pltpu.get_barrier_semaphore()
     for k in range(n_ifg - 1):
@@ -158,20 +160,17 @@
 
     def send_chunk(j):
         at, width = starts[j], widths[j]
-        for k in range(n_ifg - 1):
-            for part in range(n_track):
-                start = pl.multiple_of(ifg_target[k] * quarter + part * final + at, 128)
+        for k, part in enumerate(parts_order):
+            here = pl.ds(n_track * at + k * width, width)
+            for i in range(n_ifg - 1):
+                start = pl.multiple_of(ifg_target[i] * quarter + part * final + at, 128)
                 pltpu.make_async_remote_copy(
-                    src_ref=phases.at[0, :, pl.ds(start, width)],
-                    dst_ref=landed.at[ifg, :, pl.ds(n_track * at + part * width, width)],
-                    send_sem=z_send.at[k, j], recv_sem=z_recv.at[ifg, j],
-                    device_id={"ifg": ifg_target[k]}, device_id_type=MESH).start()
-        for part in range(n_track):
+                    src_ref=phases.at[0, :, pl.ds(start, width)], dst_ref=landed.at[ifg, :, here],
+                    send_sem=z_send.at[i, j, k], recv_sem=z_recv.at[ifg, j, k],
+                    device_id={"ifg": ifg_target[i]}, device_id_type=MESH).start()
             start = pl.multiple_of(ifg * quarter + part * final + at, 128)
             pltpu.make_async_copy(
-                phases.at[0, :, pl.ds(start, width)],
-                landed.at[ifg, :, pl.ds(n_track * at + part * width, width)],
-                z_recv.at[ifg, j]).start()
+                phases.at[0, :, pl.ds(start, width)], landed.at[ifg, :, here], z_recv.at[ifg, j, k]).start()
 
     batches = (1, min(3, len(widths)), len(widths))
     for j in range(batches[0]):
@@ -206,7 +205,9 @@
 
     knots_row = jnp.concatenate([knots[...], jnp.zeros((1, 128 - n_knots), jnp.int32)], axis=1).astype(F32)
     fitter = spline_fitter(knots_row, n_epochs, n_knots)
-    fit_hi[...], fit_lo[...] = parts(fitter, 2)
+    high, low = parts(fitter, 2)
+    fit[...] = jnp.concatenate(
+        [jnp.concatenate([high, high], axis=1), jnp.concatenate([low, jnp.zeros_like(low)], axis=1)], axis=0)
 
     look_in.wait()
     look_out[...] = look_rows[...]
@@ -284,25 +285,24 @@
     for j, width in enumerate(widths):
         if j == len(widths) - 1:
             send_mean()
-        for s in range(n_ifg):
-            chunk = landed.at[s, :, pl.ds(n_track * at, n_track * width)]
-            pltpu.make_async_copy(chunk, chunk, z_recv.at[s, j]).wait()
-        for k in range(n_track):
-            part = track_target[k] if k < n_track - 1 else track
-            where = pl.multiple_of(n_track * at + part * width, 128)
+        for k, part in enumerate(parts_order):
+            here = pl.ds(n_track * at + k * width, width)
             value = jnp.zeros((n_epochs, width), F32)
             for s in range(n_ifg):
-                phase = landed[s, :, pl.ds(where, width)]
+                chunk = landed.at[s, :, here]
+                pltpu.make_async_copy(chunk, chunk, z_recv.at[s, j, k]).wait()
+            for s in range(n_ifg):
+                phase = landed[s, :, here]
                 value = value + dot(weights[s, 0], phase) + dot(weights[s, 1], phase)
-            series[:, pl.ds(where, width)] = value
+            series[:, here] = value
             if k < n_track - 1:
                 pltpu.make_async_remote_copy(
-                    src_ref=series.at[:, pl.ds(where, width)], dst_ref=gathered.at[track, :, pl.ds(at, width)],
+                    src_ref=series.at[:, here], dst_ref=gathered.at[track, :, pl.ds(at, width)],
                     send_sem=y_send.at[k, j], recv_sem=y_recv.at[track, j],
                     device_id={"track": part}, device_id_type=MESH).start()
             else:
                 pltpu.make_async_copy(
-                    series.at[:, pl.ds(where, width)], gathered.at[track, :, pl.ds(at, width)], y_recv.at[track, j]).start()
+                    series.at[:, here], gathered.at[track, :, pl.ds(at, width)], y_recv.at[track, j]).start()
         at += width
 
     for k in range(n_track - 1):
@@ -316,9 +316,10 @@
         copy.wait_send()
     at = 0
     for j, width in enumerate(widths):
-        for k in range(n_ifg - 1):
-            chunk = landed.at[0, :, pl.ds(n_track * at, n_track * width)]
-            pltpu.make_async_copy(chunk, chunk, z_send.at[k, j]).wait()
+        for i in range(n_ifg - 1):
+            for k in range(n_track):
+                chunk = landed.at[0, :, pl.ds(0, width)]
+                pltpu.make_async_copy(chunk, chunk, z_send.at[i, j, k]).wait()
         for t in range(n_track):
             here = gathered.at[t, :, pl.ds(at, width)]
             pltpu.make_async_copy(here, here, y_recv.at[t, j]).wait()
@@ -328,7 +329,7 @@
         at += width
 
 
-def geometry_kernel(gathered, fit_hi, fit_lo, picks, table, look, means, enu, spline):
+def geometry_kernel(gathered, fit, picks, table, look, means, enu, spline):
     n_track = gathered.shape[0]
     select = picks[...]
     entries = {}
@@ -344,8 +345,8 @@
     for i in range(3):
         value = entries[i, 0] * right[0] + entries[i, 1] * right[1] + entries[i, 2] * right[2]
         enu[i] = value
-        hi, lo = parts(value, 2)
-        spline[i] = dot(fit_hi[...], hi) + dot(fit_hi[...], lo) + dot(fit_lo[...], hi)
+        both = dot(fit[...], jnp.concatenate(parts(value, 2), axis=0))
+        spline[i] = both[: both.shape[0] // 2] + both[both.shape[0] // 2 :]
 
 
 def chunk_widths(final):
@@ -370,19 +371,18 @@
     vmem = pl.BlockSpec(memory_space=pltpu.VMEM)
     anywhere = pl.BlockSpec(memory_space=pl.ANY)
     dma = pltpu.SemaphoreType.DMA
-    gathered, fit_hi, fit_lo, picks, table, look_local, means = pl.pallas_call(
+    gathered, fit, picks, table, look_local, means = pl.pallas_call(
         functools.partial(exchange_kernel, sizes),
         out_shape=(
             jax.ShapeDtypeStruct((n_track, n_epochs, final), F32),
-            jax.ShapeDtypeStruct((n_knots, n_epochs), BF16),
-            jax.ShapeDtypeStruct((n_knots, n_epochs), BF16),
+            jax.ShapeDtypeStruct((2 * n_knots, 2 * n_epochs), BF16),
             jax.ShapeDtypeStruct((n_epochs, 3 * n_masks), BF16),
             jax.ShapeDtypeStruct((len(PAIRS_OF), 3 * n_masks, final), BF16),
             jax.ShapeDtypeStruct((3, n_track, final), F32),
             jax.ShapeDtypeStruct((n_epochs, n_track), F32),
         ),
         in_specs=[anywhere, anywhere, vmem, vmem, anywhere],
-        out_specs=(anywhere,) + (vmem,) * 6,
+        out_specs=(anywhere,) + (vmem,) * 5,
         scratch_shapes=[
             pltpu.VMEM((n_ifg, 2, count), jnp.int32),
             pltpu.VMEM((count, pixels), BF16),
@@ -396,7 +396,7 @@
             pltpu.VMEM((3, n_track, final), F32),
             dma(()), dma((n_ifg,)), dma((n_ifg,)), dma((1,)),
             dma((n_pix,)), dma((n_pix,)), dma((n_ifg,)), dma((n_ifg,)),
-            dma((n_track,)), dma((n_track,)), dma((n_ifg, n)), dma((n_ifg, n)), dma((n_track, n)), dma((n_track, n)),
+            dma((n_track,)), dma((n_track,)), dma((n_ifg, n, n_track)), dma((n_ifg, n, n_track)), dma((n_track, n)), dma((n_track, n)),
         ],
         compiler_params=pltpu.CompilerParams(collective_id=0, has_side_effects=True, vmem_limit_bytes=56 << 20),
         name="exchange",
@@ -411,8 +411,7 @@
         ),
         in_specs=[
             pl.BlockSpec((n_track, n_epochs, width), lambda g: (0, 0, g)),
-            pl.BlockSpec((n_knots, n_epochs), lambda g: (0, 0)),
-            pl.BlockSpec((n_knots, n_epochs), lambda g: (0, 0)),
+            pl.BlockSpec((2 * n_knots, 2 * n_epochs), lambda g: (0, 0)),
             pl.BlockSpec((n_epochs, 3 * n_masks), lambda g: (0, 0)),
             pl.BlockSpec((len(PAIRS_OF), 3 * n_masks, width), lambda g: (0, 0, g)),
             pl.BlockSpec((3, n_track, width), lambda g: (0, 0, g)),
@@ -424,7 +423,7 @@
         ),
         compiler_params=pltpu.CompilerParams(vmem_limit_bytes=56 << 20),
         name="geometry",
-    )(gathered, fit_hi, fit_lo, picks, table, look_local, means)
+    )(gathered, fit, picks, table, look_local, means)
     return enu, spline
 
 

time: 150 us -> 142 us (0.947)
  Pallas kernels: 149 us -> 141 us
    pallas_call x1, Pallas kernels: 142 us -> 134 us  [shards(): pl.pallas_call(functools.partial(exchange_kernel, sizes), out_shape=(jax....]
where the time goes in v3:
time: 142 us
  Pallas kernels  141 us (99%)
    pallas_call x1, Pallas kernels, shards(): pl.pallas_call(functools.partial(exchange_kernel, sizes), out_shape=(jax....  134 us
    pallas_call x1, Pallas kernels, shards(): pl.pallas_call(geometry_kernel, grid=(final // width,), out_shape=(jax.Sh...  6.89 us

profile of v3, /device:TPU:1, one launch (start us, length us, event | category | flops | bytes accessed | tf_op | source)
XLA Modules:
  0.0 141.8 jit_solution(7488030909952177543)
XLA Ops:
  0.6 134.3 %exchange.1 = (f32[4,320,1024]{2,1,0:T(8,128)}, bf16[64,640]{1,0:T(8,128)(2,1)}, bf16[320,48]{1,0:T(8,128)(2,1)}, bf16[6,48,1024]{2,1,0:T(8,128)(2,1)}, f32[3,4,1024]{2,1,0:T(4,128)}, /*index=5*/f32[320,4]{1,0:T(8,128)}) custom-call(bf16[1,150,16384]{2,1,0:T(8,128)(2,1)} %phases.1, s32[1,2,150]{2,1,0:T(2,128)} %bitcast.4, s32[4,250]{1,0:T(4,128)} %date_map.1, ...), custom_call_target="tpu_custom_call" | custom-call | tf_op jit(solution)/shard_map/exchange/pallas_call | solution.py:374
  134.9 6.9 %geometry.1 = (f32[3,320,1024]{2,1,0:T(8,128)}, f32[3,32,1024]{2,1,0:T(8,128)}) custom-call(f32[4,320,1024]{2,1,0:T(8,128)} %get-tuple-element.8.gathered, bf16[64,640]{1,0:T(8,128)(2,1)} %get-tuple-element.9.fit, bf16[320,48]{1,0:T(8,128)(2,1)} %get-tuple-element.10.picks, bf16[6,48,1024]{2,1,0:T(8,128)(2,1)} %get-tuple-element.11.table, ...), custom_call_target="tpu_custom_call" | custom-call | tf_op jit(solution)/shard_map/geometry/pallas_call | solution.py:405

commit v4 on v3

--- a/solution.py
+++ b/solution.py
@@ -15,6 +15,9 @@
 damping = 0.5
 ridge = 0.1
 BAND = 8
+AHEAD_FIRST = 6
+AHEAD = 3
+MEAN_PIECE = 7
 PAIRS_OF = ((0, 0), (0, 1), (0, 2), (1, 1), (1, 2), (2, 2))
 
 
@@ -121,6 +124,7 @@
     own_sem, pair_send, pair_recv, look_sem, sum_send, sum_recv, total_send, total_recv, mean_send, mean_recv, z_send, z_recv, y_send, y_recv,
 ):
     n_track, n_ifg, n_pix, widths, n_dates, n_epochs, n_knots = sizes
+    ahead_first, ahead, mean_piece = AHEAD_FIRST, AHEAD, min(MEAN_PIECE, n_track * len(widths) - 5)
     track, ifg, pix = lax.axis_index("track"), lax.axis_index("ifg"), lax.axis_index("pix")
     count, pixels = phases.shape[1], phases.shape[2]
     quarter = pixels // n_ifg
@@ -158,23 +162,32 @@
     look_in.start()
     starts = [sum(widths[:j]) for j in range(len(widths))]
 
-    def send_chunk(j):
-        at, width = starts[j], widths[j]
-        for k, part in enumerate(parts_order):
-            here = pl.ds(n_track * at + k * width, width)
-            for i in range(n_ifg - 1):
-                start = pl.multiple_of(ifg_target[i] * quarter + part * final + at, 128)
-                pltpu.make_async_remote_copy(
-                    src_ref=phases.at[0, :, pl.ds(start, width)], dst_ref=landed.at[ifg, :, here],
-                    send_sem=z_send.at[i, j, k], recv_sem=z_recv.at[ifg, j, k],
-                    device_id={"ifg": ifg_target[i]}, device_id_type=MESH).start()
-            start = pl.multiple_of(ifg * quarter + part * final + at, 128)
-            pltpu.make_async_copy(
-                phases.at[0, :, pl.ds(start, width)], landed.at[ifg, :, here], z_recv.at[ifg, j, k]).start()
-
-    batches = (1, min(3, len(widths)), len(widths))
-    for j in range(batches[0]):
-        send_chunk(j)
+    tail = max(len(widths) - 2, 0)
+    order = [(j, k) for j in range(tail) for k in range(n_track)]
+    order += [(j, k) for k in range(n_track) for j in range(tail, len(widths))]
+
+    def send_piece(j, k):
+        at, width, part = starts[j], widths[j], parts_order[k]
+        here = pl.ds(n_track * at + k * width, width)
+        for i in range(n_ifg - 1):
+            start = pl.multiple_of(ifg_target[i] * quarter + part * final + at, 128)
+            pltpu.make_async_remote_copy(
+                src_ref=phases.at[0, :, pl.ds(start, width)], dst_ref=landed.at[ifg, :, here],
+                send_sem=z_send.at[i, j, k], recv_sem=z_recv.at[ifg, j, k],
+                device_id={"ifg": ifg_target[i]}, device_id_type=MESH).start()
+        start = pl.multiple_of(ifg * quarter + part * final + at, 128)
+        pltpu.make_async_copy(
+            phases.at[0, :, pl.ds(start, width)], landed.at[ifg, :, here], z_recv.at[ifg, j, k]).start()
+
+    ends = [sum(widths[j] for j, _ in order[: p + 1]) for p in range(len(order))]
+    queued = [0]
+
+    def send_upto(reach):
+        while queued[0] < len(order) and ends[queued[0]] <= reach:
+            send_piece(*order[queued[0]])
+            queued[0] += 1
+
+    send_upto(final)
 
     own_copy.wait()
     piece = 1024 if pixels % 1024 == 0 else pixels
@@ -200,8 +213,7 @@
             src_ref=sums.at[0], dst_ref=sums.at[k], send_sem=sum_send.at[k], recv_sem=sum_recv.at[k],
             device_id={"pix": lax.rem(pix + k, n_pix)}, device_id_type=MESH))
         sum_copies[-1].start()
-    for j in range(batches[0], batches[1]):
-        send_chunk(j)
+    send_upto(ahead_first * final // 4)
 
     knots_row = jnp.concatenate([knots[...], jnp.zeros((1, 128 - n_knots), jnp.int32)], axis=1).astype(F32)
     fitter = spline_fitter(knots_row, n_epochs, n_knots)
@@ -262,8 +274,6 @@
             src_ref=totals.at[ifg], dst_ref=totals.at[ifg], send_sem=total_send.at[k], recv_sem=total_recv.at[ifg],
             device_id={"ifg": ifg_target[k]}, device_id_type=MESH))
         total_copies[-1].start()
-    for j in range(batches[1], batches[2]):
-        send_chunk(j)
 
     def send_mean():
         for k in range(n_ifg - 1):
@@ -281,36 +291,38 @@
             mean_copies[-1].start()
 
     mean_copies = []
-    at = 0
-    for j, width in enumerate(widths):
-        if j == len(widths) - 1:
+    def mean_columns():
+        for k in range(n_track - 1):
+            t = track_target[k]
+            pltpu.make_async_copy(means.at[t], means.at[t], mean_recv.at[t]).wait()
+        eye = (iota((n_epochs, n_epochs), 0) == iota((n_epochs, n_epochs), 1)).astype(F32)
+        mean_out[...] = jnp.concatenate(
+            [dot(eye, means[t], ((1,), (1,)), precision=HIGH) for t in range(n_track)], axis=1)
+
+    for at_piece, (j, k) in enumerate(order):
+        at, width, part = starts[j], widths[j], parts_order[k]
+        if at_piece == mean_piece:
             send_mean()
-        for k, part in enumerate(parts_order):
-            here = pl.ds(n_track * at + k * width, width)
-            value = jnp.zeros((n_epochs, width), F32)
-            for s in range(n_ifg):
-                chunk = landed.at[s, :, here]
-                pltpu.make_async_copy(chunk, chunk, z_recv.at[s, j, k]).wait()
-            for s in range(n_ifg):
-                phase = landed[s, :, here]
-                value = value + dot(weights[s, 0], phase) + dot(weights[s, 1], phase)
-            series[:, here] = value
-            if k < n_track - 1:
-                pltpu.make_async_remote_copy(
-                    src_ref=series.at[:, here], dst_ref=gathered.at[track, :, pl.ds(at, width)],
-                    send_sem=y_send.at[k, j], recv_sem=y_recv.at[track, j],
-                    device_id={"track": part}, device_id_type=MESH).start()
-            else:
-                pltpu.make_async_copy(
-                    series.at[:, here], gathered.at[track, :, pl.ds(at, width)], y_recv.at[track, j]).start()
-        at += width
-
-    for k in range(n_track - 1):
-        t = track_target[k]
-        pltpu.make_async_copy(means.at[t], means.at[t], mean_recv.at[t]).wait()
-    eye = (iota((n_epochs, n_epochs), 0) == iota((n_epochs, n_epochs), 1)).astype(F32)
-    mean_out[...] = jnp.concatenate(
-        [dot(eye, means[t], ((1,), (1,)), precision=HIGH) for t in range(n_track)], axis=1)
+        if at_piece == max(len(order) - 4, mean_piece + 1):
+            mean_columns()
+        here = pl.ds(n_track * at + k * width, width)
+        for s in range(n_ifg):
+            chunk = landed.at[s, :, here]
+            pltpu.make_async_copy(chunk, chunk, z_recv.at[s, j, k]).wait()
+        send_upto(n_track * final if at_piece == len(order) - 1 else ends[at_piece] + ahead * final // 4)
+        value = jnp.zeros((n_epochs, width), F32)
+        for s in range(n_ifg):
+            phase = landed[s, :, here]
+            value = value + dot(weights[s, 0], phase) + dot(weights[s, 1], phase)
+        series[:, here] = value
+        if k < n_track - 1:
+            pltpu.make_async_remote_copy(
+                src_ref=series.at[:, here], dst_ref=gathered.at[track, :, pl.ds(at, width)],
+                send_sem=y_send.at[k, j], recv_sem=y_recv.at[track, j],
+                device_id={"track": part}, device_id_type=MESH).start()
+        else:
+            pltpu.make_async_copy(
+                series.at[:, here], gathered.at[track, :, pl.ds(at, width)], y_recv.at[track, j]).start()
 
     for copy in pair_copies + sum_copies + total_copies + mean_copies:
         copy.wait_send()

time: 142 us -> 136 us (0.958)
  Pallas kernels: 141 us -> 135 us
    pallas_call x1, Pallas kernels: 134 us -> 128 us  [shards(): pl.pallas_call(functools.partial(exchange_kernel, sizes), out_shape=(jax....]
where the time goes in v4:
time: 136 us; the launch traced here: 135 us
  Pallas kernels  135 us (99%)
    pallas_call x1, Pallas kernels, shards(): pl.pallas_call(functools.partial(exchange_kernel, sizes), out_shape=(jax....  128 us
    pallas_call x1, Pallas kernels, shards(): pl.pallas_call(geometry_kernel, grid=(final // width,), out_shape=(jax.Sh...  6.9 us

profile of v4, /device:TPU:1, one launch (start us, length us, event | category | flops | bytes accessed | tf_op | source)
XLA Modules:
  0.0 135.2 jit_solution(12744803619952361448)
XLA Ops:
  0.6 127.6 %exchange.1 = (f32[4,320,1024]{2,1,0:T(8,128)}, bf16[64,640]{1,0:T(8,128)(2,1)}, bf16[320,48]{1,0:T(8,128)(2,1)}, bf16[6,48,1024]{2,1,0:T(8,128)(2,1)}, f32[3,4,1024]{2,1,0:T(4,128)}, /*index=5*/f32[320,4]{1,0:T(8,128)}) custom-call(bf16[1,150,16384]{2,1,0:T(8,128)(2,1)} %phases.1, s32[1,2,150]{2,1,0:T(2,128)} %bitcast.4, s32[4,250]{1,0:T(4,128)} %date_map.1, ...), custom_call_target="tpu_custom_call" | custom-call | tf_op jit(solution)/shard_map/exchange/pallas_call | solution.py:386
  128.3 6.9 %geometry.1 = (f32[3,320,1024]{2,1,0:T(8,128)}, f32[3,32,1024]{2,1,0:T(8,128)}) custom-call(f32[4,320,1024]{2,1,0:T(8,128)} %get-tuple-element.8.gathered, bf16[64,640]{1,0:T(8,128)(2,1)} %get-tuple-element.9.fit, bf16[320,48]{1,0:T(8,128)(2,1)} %get-tuple-element.10.picks, bf16[6,48,1024]{2,1,0:T(8,128)(2,1)} %get-tuple-element.11.table, ...), custom_call_target="tpu_custom_call" | custom-call | tf_op jit(solution)/shard_map/geometry/pallas_call | solution.py:417

commit v5 on v4

--- a/solution.py
+++ b/solution.py
@@ -15,6 +15,7 @@
 damping = 0.5
 ridge = 0.1
 BAND = 8
+FIRST = 4
 AHEAD_FIRST = 6
 AHEAD = 3
 MEAN_PIECE = 7
@@ -121,10 +122,10 @@
     sizes, phases, pairs, date_map, knots, look,
     gathered, fit, picks, table, look_out, mean_out,
     pair_all, own, landed, weights, incid, series, sums, totals, means, look_rows,
-    own_sem, pair_send, pair_recv, look_sem, sum_send, sum_recv, total_send, total_recv, mean_send, mean_recv, z_send, z_recv, y_send, y_recv,
+    go, ready, own_sem, pair_send, pair_recv, look_sem, sum_send, sum_recv, total_send, total_recv, mean_send, mean_recv, z_send, z_recv, y_send, y_recv,
 ):
     n_track, n_ifg, n_pix, widths, n_dates, n_epochs, n_knots = sizes
-    ahead_first, ahead, mean_piece = AHEAD_FIRST, AHEAD, min(MEAN_PIECE, n_track * len(widths) - 5)
+    first, ahead_first, ahead, mean_piece = FIRST, AHEAD_FIRST, AHEAD, min(MEAN_PIECE, n_track * len(widths) - 5)
     track, ifg, pix = lax.axis_index("track"), lax.axis_index("ifg"), lax.axis_index("pix")
     count, pixels = phases.shape[1], phases.shape[2]
     quarter = pixels // n_ifg
@@ -139,14 +140,38 @@
     track_target = [lax.rem(track + k, n_track) for k in steps]
     parts_order = track_target + [track]
 
+    middle, helper = 1, 0
+    others = [i for i in range(n_ifg) if i != middle]
+    is_middle = ifg == middle
     barrier = pltpu.get_barrier_semaphore()
-    for k in range(n_ifg - 1):
-        pl.semaphore_signal(barrier, inc=1, device_id={"ifg": ifg_target[k]}, device_id_type=MESH)
-    for k in range(n_track - 1):
-        pl.semaphore_signal(barrier, inc=1, device_id={"track": track_target[k]}, device_id_type=MESH)
-    for k in range(1, n_pix):
-        pl.semaphore_signal(barrier, inc=1, device_id={"pix": lax.rem(pix + k, n_pix)}, device_id_type=MESH)
-    pl.semaphore_wait(barrier, n_ifg + n_track + n_pix - 3)
+
+    @pl.when(is_middle)
+    def _():
+        pl.semaphore_wait(barrier, n_ifg - 1)
+        for i in others:
+            pl.semaphore_signal(go, inc=1, device_id={"ifg": i}, device_id_type=MESH)
+
+    @pl.when(jnp.logical_not(is_middle))
+    def _():
+        pl.semaphore_signal(barrier, inc=1, device_id={"ifg": middle}, device_id_type=MESH)
+        pl.semaphore_wait(go, 1)
+        for k in range(n_track - 1):
+            pl.semaphore_signal(barrier, inc=1, device_id={"track": track_target[k]}, device_id_type=MESH)
+        for k in range(1, n_pix):
+            pl.semaphore_signal(barrier, inc=1, device_id={"pix": lax.rem(pix + k, n_pix)}, device_id_type=MESH)
+
+    def wait_for_peers():
+        @pl.when(jnp.logical_not(is_middle))
+        def _():
+            pl.semaphore_wait(barrier, n_track + n_pix - 2)
+
+        @pl.when(ifg == helper)
+        def _():
+            pl.semaphore_signal(ready, inc=1, device_id={"ifg": middle}, device_id_type=MESH)
+
+        @pl.when(is_middle)
+        def _():
+            pl.semaphore_wait(ready, 1)
 
     own_copy = pltpu.make_async_copy(phases.at[0], own, own_sem)
     own_copy.start()
@@ -187,7 +212,7 @@
             send_piece(*order[queued[0]])
             queued[0] += 1
 
-    send_upto(final)
+    send_upto(first * final // 4)
 
     own_copy.wait()
     piece = 1024 if pixels % 1024 == 0 else pixels
@@ -206,14 +231,6 @@
     n_masks = 1 << n_track
     lane = iota((n_epochs, 3 * n_masks), 1)
     picks[...] = (lane % n_masks == code).astype(F32).astype(BF16)
-
-    sum_copies = []
-    for k in range(1, n_pix):
-        sum_copies.append(pltpu.make_async_remote_copy(
-            src_ref=sums.at[0], dst_ref=sums.at[k], send_sem=sum_send.at[k], recv_sem=sum_recv.at[k],
-            device_id={"pix": lax.rem(pix + k, n_pix)}, device_id_type=MESH))
-        sum_copies[-1].start()
-    send_upto(ahead_first * final // 4)
 
     knots_row = jnp.concatenate([knots[...], jnp.zeros((1, 128 - n_knots), jnp.int32)], axis=1).astype(F32)
     fitter = spline_fitter(knots_row, n_epochs, n_knots)
@@ -242,6 +259,15 @@
     det = a00 * c00 + a01 * c01 + a02 * c02
     for e, cofactor in enumerate((c00, c01, c02, c11, c12, c22)):
         table[e] = jnp.concatenate(parts(cofactor / det, 3), axis=0)
+
+    wait_for_peers()
+    sum_copies = []
+    for k in range(1, n_pix):
+        sum_copies.append(pltpu.make_async_remote_copy(
+            src_ref=sums.at[0], dst_ref=sums.at[k], send_sem=sum_send.at[k], recv_sem=sum_recv.at[k],
+            device_id={"pix": lax.rem(pix + k, n_pix)}, device_id_type=MESH))
+        sum_copies[-1].start()
+    send_upto(ahead_first * final // 4)
 
     for s in range(n_ifg):
         pltpu.make_async_copy(pair_all.at[s], pair_all.at[s], pair_recv.at[s]).wait()
@@ -406,6 +432,7 @@
             pltpu.VMEM((n_ifg, 1, count), F32),
             pltpu.VMEM((n_track, 1, n_epochs), F32),
             pltpu.VMEM((3, n_track, final), F32),
+            pltpu.SemaphoreType.REGULAR, pltpu.SemaphoreType.REGULAR,
             dma(()), dma((n_ifg,)), dma((n_ifg,)), dma((1,)),
             dma((n_pix,)), dma((n_pix,)), dma((n_ifg,)), dma((n_ifg,)),
             dma((n_track,)), dma((n_track,)), dma((n_ifg, n, n_track)), dma((n_ifg, n, n_track)), dma((n_track, n)), dma((n_track, n)),

time: 136 us -> 131 us (0.963)
  Pallas kernels: 135 us -> 129 us
    pallas_call x1, Pallas kernels: 128 us -> 122 us  [shards(): pl.pallas_call(functools.partial(exchange_kernel, sizes), out_shape=(jax....]
where the time goes in v5:
time: 131 us; the launch traced here: 130 us
  Pallas kernels  129 us (98%)
    pallas_call x1, Pallas kernels, shards(): pl.pallas_call(functools.partial(exchange_kernel, sizes), out_shape=(jax....  122 us
    pallas_call x1, Pallas kernels, shards(): pl.pallas_call(geometry_kernel, grid=(final // width,), out_shape=(jax.Sh...  6.88 us

profile of v5, /device:TPU:1, one launch (start us, length us, event | category | flops | bytes accessed | tf_op | source)
XLA Modules:
  0.0 130.0 jit_solution(17455948430786419166)
XLA Ops:
  0.6 122.5 %exchange.1 = (f32[4,320,1024]{2,1,0:T(8,128)}, bf16[64,640]{1,0:T(8,128)(2,1)}, bf16[320,48]{1,0:T(8,128)(2,1)}, bf16[6,48,1024]{2,1,0:T(8,128)(2,1)}, f32[3,4,1024]{2,1,0:T(4,128)}, /*index=5*/f32[320,4]{1,0:T(8,128)}) custom-call(bf16[1,150,16384]{2,1,0:T(8,128)(2,1)} %phases.1, s32[1,2,150]{2,1,0:T(2,128)} %bitcast.4, s32[4,250]{1,0:T(4,128)} %date_map.1, ...), custom_call_target="tpu_custom_call" | custom-call | tf_op jit(solution)/shard_map/exchange/pallas_call | solution.py:412
  123.1 6.9 %geometry.1 = (f32[3,320,1024]{2,1,0:T(8,128)}, f32[3,32,1024]{2,1,0:T(8,128)}) custom-call(f32[4,320,1024]{2,1,0:T(8,128)} %get-tuple-element.8.gathered, bf16[64,640]{1,0:T(8,128)(2,1)} %get-tuple-element.9.fit, bf16[320,48]{1,0:T(8,128)(2,1)} %get-tuple-element.10.picks, bf16[6,48,1024]{2,1,0:T(8,128)(2,1)} %get-tuple-element.11.table, ...), custom_call_target="tpu_custom_call" | custom-call | tf_op jit(solution)/shard_map/geometry/pallas_call | solution.py:444

commit v6 on v5

--- a/solution.py
+++ b/solution.py
@@ -387,6 +387,10 @@
         spline[i] = both[: both.shape[0] // 2] + both[both.shape[0] // 2 :]
 
 
+def stay(value):
+    return pltpu.with_memory_space_constraint(value, pltpu.HBM)
+
+
 def chunk_widths(final):
     if final == 1024:
         return (256, 256, 256, 128, 128)
@@ -408,6 +412,7 @@
     sizes = (n_track, n_ifg, n_pix, widths, n_dates, n_epochs, n_knots)
     vmem = pl.BlockSpec(memory_space=pltpu.VMEM)
     anywhere = pl.BlockSpec(memory_space=pl.ANY)
+    outside = pl.BlockSpec(memory_space=pltpu.HBM)
     dma = pltpu.SemaphoreType.DMA
     gathered, fit, picks, table, look_local, means = pl.pallas_call(
         functools.partial(exchange_kernel, sizes),
@@ -419,7 +424,7 @@
             jax.ShapeDtypeStruct((3, n_track, final), F32),
             jax.ShapeDtypeStruct((n_epochs, n_track), F32),
         ),
-        in_specs=[anywhere, anywhere, vmem, vmem, anywhere],
+        in_specs=[outside, outside, vmem, vmem, outside],
         out_specs=(anywhere,) + (vmem,) * 5,
         scratch_shapes=[
             pltpu.VMEM((n_ifg, 2, count), jnp.int32),
@@ -437,9 +442,9 @@
             dma((n_pix,)), dma((n_pix,)), dma((n_ifg,)), dma((n_ifg,)),
             dma((n_track,)), dma((n_track,)), dma((n_ifg, n, n_track)), dma((n_ifg, n, n_track)), dma((n_track, n)), dma((n_track, n)),
         ],
-        compiler_params=pltpu.CompilerParams(collective_id=0, has_side_effects=True, vmem_limit_bytes=56 << 20),
+        compiler_params=pltpu.CompilerParams(collective_id=0, has_side_effects=True, vmem_limit_bytes=28 << 20),
         name="exchange",
-    )(phases, jnp.transpose(pairs, (0, 2, 1)), date_map, knots[None, :], jnp.transpose(look, (1, 0, 2)))
+    )(stay(phases), stay(jnp.transpose(pairs, (0, 2, 1))), stay(date_map), stay(knots[None, :]), stay(jnp.transpose(look, (1, 0, 2))))
     width = min(final, 256)
     enu, spline = pl.pallas_call(
         geometry_kernel,
@@ -460,7 +465,7 @@
             pl.BlockSpec((3, n_epochs, width), lambda g: (0, 0, g)),
             pl.BlockSpec((3, n_knots, width), lambda g: (0, 0, g)),
         ),
-        compiler_params=pltpu.CompilerParams(vmem_limit_bytes=56 << 20),
+        compiler_params=pltpu.CompilerParams(vmem_limit_bytes=20 << 20),
         name="geometry",
     )(gathered, fit, picks, table, look_local, means)
     return enu, spline

time: 131 us -> 128 us (0.977)
  Pallas kernels: 129 us -> 127 us
    pallas_call x1, Pallas kernels: 6.88 us -> 5.19 us  [shards(): pl.pallas_call(geometry_kernel, grid=(final // width,), out_shape=(jax.Sh...]
where the time goes in v6:
time: 128 us; the launch traced here: 127 us
  Pallas kernels  127 us (99%)
    pallas_call x1, Pallas kernels, shards(): pl.pallas_call(functools.partial(exchange_kernel, sizes), out_shape=(jax....  121 us
    pallas_call x1, Pallas kernels, shards(): pl.pallas_call(geometry_kernel, grid=(final // width,), out_shape=(jax.Sh...  5.19 us

profile of v6, /device:TPU:1, one launch (start us, length us, event | category | flops | bytes accessed | tf_op | source)
XLA Modules:
  0.0 127.2 jit_solution(3427630996029877678)
XLA Ops:
  0.6 121.4 %exchange.1 = (f32[4,320,1024]{2,1,0:T(8,128)S(1)}, bf16[64,640]{1,0:T(8,128)(2,1)S(1)}, bf16[320,48]{1,0:T(8,128)(2,1)S(1)}, bf16[6,48,1024]{2,1,0:T(8,128)(2,1...) custom-call(bf16[1,150,16384]{2,1,0:T(8,128)(2,1)} %phases.1, s32[1,2,150]{2,1,0:T(2,128)} %bitcast.4, ...), custom_call_target="tpu_custom_call" | custom-call | tf_op jit(solution)/shard_map/exchange/pallas_call | solution.py:417
  122.0 5.2 %geometry.1 = (f32[3,320,1024]{2,1,0:T(8,128)}, f32[3,32,1024]{2,1,0:T(8,128)}) custom-call(f32[4,320,1024]{2,1,0:T(8,128)S(1)} %get-tuple-element.8.gathered, bf16[64,640]{1,0:T(8,128)(2,1)S(1)} %get-tuple-element.9.fit, bf16[320,48]{1,0:T(8,128)(2,1)S(1)} %get-tuple-element.10.picks, bf16[6,48,1024]{2,1,0:T(8,128)(2,1)S(1)} %get-tuple-element.11.table, ...), custom_call_target="tpu_custom_call" | custom-call | tf_op jit(solution)/shard_map/geometry/pallas_call | solution.py:449

commit v7 on v6

--- a/solution.py
+++ b/solution.py
@@ -17,7 +17,7 @@
 BAND = 8
 FIRST = 4
 AHEAD_FIRST = 6
-AHEAD = 3
+AHEAD = 2
 MEAN_PIECE = 7
 PAIRS_OF = ((0, 0), (0, 1), (0, 2), (1, 1), (1, 2), (2, 2))
 

time: 128 us -> 127 us (level)
  Pallas kernels: 127 us -> 125 us
    pallas_call x1, Pallas kernels: 121 us -> 120 us  [shards(): pl.pallas_call(functools.partial(exchange_kernel, sizes), out_shape=(jax....]
where the time goes in v7:
time: 127 us; the launch traced here: 125 us
  Pallas kernels  125 us (98%)
    pallas_call x1, Pallas kernels, shards(): pl.pallas_call(functools.partial(exchange_kernel, sizes), out_shape=(jax....  120 us
    pallas_call x1, Pallas kernels, shards(): pl.pallas_call(geometry_kernel, grid=(final // width,), out_shape=(jax.Sh...  5.18 us

profile of v7, /device:TPU:1, one launch (start us, length us, event | category | flops | bytes accessed | tf_op | source)
XLA Modules:
  0.0 125.4 jit_solution(11040520977810363096)
XLA Ops:
  0.6 119.6 %exchange.1 = (f32[4,320,1024]{2,1,0:T(8,128)S(1)}, bf16[64,640]{1,0:T(8,128)(2,1)S(1)}, bf16[320,48]{1,0:T(8,128)(2,1)S(1)}, bf16[6,48,1024]{2,1,0:T(8,128)(2,1...) custom-call(bf16[1,150,16384]{2,1,0:T(8,128)(2,1)} %phases.1, s32[1,2,150]{2,1,0:T(2,128)} %bitcast.4, ...), custom_call_target="tpu_custom_call" | custom-call | tf_op jit(solution)/shard_map/exchange/pallas_call | solution.py:417
  120.2 5.2 %geometry.1 = (f32[3,320,1024]{2,1,0:T(8,128)}, f32[3,32,1024]{2,1,0:T(8,128)}) custom-call(f32[4,320,1024]{2,1,0:T(8,128)S(1)} %get-tuple-element.8.gathered, bf16[64,640]{1,0:T(8,128)(2,1)S(1)} %get-tuple-element.9.fit, bf16[320,48]{1,0:T(8,128)(2,1)S(1)} %get-tuple-element.10.picks, bf16[6,48,1024]{2,1,0:T(8,128)(2,1)S(1)} %get-tuple-element.11.table, ...), custom_call_target="tpu_custom_call" | custom-call | tf_op jit(solution)/shard_map/geometry/pallas_call | solution.py:449
